TPU v7x, 1024 devices: a whole 4x8x16 slice. The times are simulated.
1024 devices in a mesh: grp: 4 (over x), dom: 16 (over z_lo, core), pen: 16 (over z_hi, y).
Axes of the slice: x: 4, y: 8, z: 16 (z_hi: 2, z_lo: 8; z = z_hi * 8 + z_lo), core: 2. Of those that a mesh axis runs over, the one named last changes fastest.
Arguments:
- atoms: float32 [4, 4, 16, 65536], P(None, 'grp', 'dom', 'pen'), may hold values from -6 to 6, as said below
- pair_home: int32 [4, 16, 1024], P('grp', 'dom', 'pen'), may hold values from 0 to 31
- pair_other: int32 [4, 16, 1024], P('grp', 'dom', 'pen'), may hold values from 0 to 287
Outputs:
- short_forces: float32 [3, 4, 16, 65536], P(None, 'grp', 'dom', 'pen')
- long_forces: float32 [3, 4, 16, 65536], P(None, 'grp', 'dom', 'pen')
Inputs may be any that keep to these rules, and one draw needn't show every extreme that they name: `atoms`: in block (g, d, p) the first coordinate lies in [d / 16, (d + 0.98) / 16), the second in [p / 16, (p + 0.98) / 16), the third in [0, 1); the fourth component is the charge, within -6 to 6.
All inputs are finite; a program needn't handle non-finite values.
Results may differ from a plain program's by a relative error of at most 0.0003.
Values sent between devices are 32-bit elements; how exact they have to be, the bound alone decides.
A program may use at most 32 MiB of HBM per device.

v0:
```python
import math

import jax
import jax.numpy as jnp
from jax import lax
from jax.sharding import PartitionSpec as P

NG = 128
TILE = 128


exact_precision = lax.Precision.HIGHEST


def with_halo(block, sides, width):
    for axis, dim in sides:
        count = lax.axis_size(axis)
        forward = [(i, i + 1) for i in range(count - 1)]
        forward.append((count - 1, 0))
        backward = [(target, source) for source, target in forward]
        low = lax.ppermute(
            lax.slice_in_dim(block, block.shape[dim] - width, None, axis=dim), axis, forward
        )
        high = lax.ppermute(lax.slice_in_dim(block, 0, width, axis=dim), axis, backward)
        block = jnp.concatenate([low, block, high], axis=dim)
    return block


def in_blocks(array, dim, size):
    before, after = (array.shape[:dim], array.shape[dim + 1 :])
    return jnp.moveaxis(array.reshape(*before, size, -1, *after), dim, 0)


def summed_on_arrival(array, axis, dim):
    pieces = in_blocks(array, dim, lax.axis_size(axis))
    arrived = lax.all_to_all(pieces, axis, split_axis=0, concat_axis=0, tiled=True)
    return arrived.sum(axis=0)


def in_one_piece(arrays, axis, dim, along):
    both = jnp.concatenate(arrays, axis=along)
    filled, at, finished = (summed_on_arrival(both, axis, dim), 0, [])
    for a in arrays:
        finished.append(lax.slice_in_dim(filled, at, at + a.shape[along], axis=along))
        at += a.shape[along]
    return tuple(finished)


def side_by_side(arrays, axis, split_dim, concat_dim, along):
    ends, at = ([], 0)
    for a in arrays[:-1]:
        at += a.shape[along]
        ends.append(at)
    both = jnp.concatenate(arrays, axis=along)
    return tuple(
        jnp.split(
            lax.all_to_all(both, axis, split_axis=split_dim, concat_axis=concat_dim, tiled=True),
            ends,
            axis=along,
        )
    )


def rows_first(arrays, axis, dims):
    turned = [jnp.moveaxis(a, dim, 0) for a, dim in zip(arrays, dims)]
    widths = [t[0].size for t in turned]
    both = jnp.concatenate([t.reshape(-1, w) for t, w in zip(turned, widths)], axis=1)
    filled = lax.all_gather(both, axis, axis=0, tiled=True)
    pieces = jnp.split(filled, [sum(widths[:k]) for k in range(1, len(widths))], axis=1)
    return tuple(
        (
            jnp.moveaxis(b.reshape(-1, *t.shape[1:]), 0, dim)
            for b, t, dim in zip(pieces, turned, dims)
        )
    )


def passed_along(block, axis, distance):
    devices = range(lax.axis_size(axis))
    route = [((i - distance) % len(devices), i) for i in devices]
    return lax.ppermute(block, axis, route)


def matmul(left, right):
    return jnp.dot(left, right, precision=exact_precision, preferred_element_type=jnp.float32)


def spline_terms(scaled):
    floored = jnp.floor(scaled)
    fraction = scaled - floored
    remain = 1.0 - fraction
    frac_sq = fraction * fraction
    frac_cube = frac_sq * fraction
    thetas = [
        remain * remain * remain / 6.0,
        (3.0 * frac_cube - 6.0 * frac_sq + 4.0) / 6.0,
        (-3.0 * frac_cube + 3.0 * frac_sq + 3.0 * fraction + 1.0) / 6.0,
        frac_cube / 6.0,
    ]
    slopes = [
        -0.5 * remain * remain,
        1.5 * frac_sq - 2.0 * fraction,
        -1.5 * frac_sq + fraction + 0.5,
        0.5 * frac_sq,
    ]
    return (floored.astype(jnp.int32) - 3, thetas, slopes)


def spline_rows(coords, anchor, planes, grid_cells):
    lowest, thetas, slopes = spline_terms(coords * grid_cells)
    plane_ids = lax.broadcasted_iota(jnp.int32, (planes, 1), 0)
    values = jnp.zeros((planes, coords.shape[0]), jnp.float32)
    slopes_out = jnp.zeros_like(values)
    for offset in range(4):
        matches = (jnp.mod(lowest + offset - anchor, grid_cells)[None, :] == plane_ids).astype(
            jnp.float32
        )
        values = values + matches * thetas[offset][None, :]
        slopes_out = slopes_out + matches * slopes[offset][None, :]
    return (values, slopes_out)


def pair_push(home_pos, other_pos, scales):
    displace = home_pos[:, :3, :, None] - other_pos[:, :3, None, :]
    displace = displace - jnp.floor(displace + 0.5)
    scaled = displace * scales[None, :, None, None]
    weight = jnp.exp(-0.5 * jnp.sum(scaled * scaled, axis=1)) * other_pos[:, 3, None, :]
    return jnp.sum(scaled * weight[:, None], axis=3) * home_pos[:, 3:4, :]


def green_factor(freq_x, freq_y, freq_z, grid_cells):

    def signed(frequencies):
        return jnp.where(frequencies < grid_cells // 2, frequencies, frequencies - grid_cells)

    def modulus(frequencies):
        turned = 2.0 * jnp.pi * signed(frequencies).astype(jnp.float32) / grid_cells
        ratio = (2.0 + jnp.cos(turned)) / 3.0
        return 1.0 / (ratio * ratio)

    signed_x = signed(freq_x)
    signed_y = signed(freq_y)
    signed_z = signed(freq_z)
    square = (signed_x * signed_x + signed_y * signed_y + signed_z * signed_z).astype(jnp.float32)
    beta = 0.6 * grid_cells
    safe = jnp.maximum(square, 1.0)
    value = jnp.exp(-jnp.pi * jnp.pi * square / (beta * beta)) / (jnp.pi * safe)
    value = value * modulus(freq_x) * modulus(freq_y) * modulus(freq_z)
    return jnp.where(square > 0.5, value, 0.0)


def phase_tables(frequencies, cell_ids, grid_cells):
    turns = jnp.mod(frequencies[:, None] * cell_ids[None, :], grid_cells).astype(jnp.float32)
    angle = turns * (2.0 * jnp.pi / grid_cells)
    return (jnp.cos(angle), jnp.sin(angle))


def spread_mesh(spread_atoms, first_x, first_y, slab_cells, column, grid_cells):
    span_size = min(1024, spread_atoms.shape[1])
    batches = spread_atoms.reshape(4, -1, span_size).transpose(1, 0, 2)

    def spread_step(totals, atom_batch):
        weight_x, unused_x = spline_rows(atom_batch[0], first_x, slab_cells, grid_cells)
        weight_y, unused_y = spline_rows(atom_batch[1], first_y, column, grid_cells)
        weight_z, unused_z = spline_rows(atom_batch[2], 0, grid_cells, grid_cells)
        weighted_y = weight_y * atom_batch[3][None, :]
        paired = weight_x[:, None, :] * weighted_y[None, :, :]
        paired = paired.reshape(slab_cells * column, span_size)
        product = lax.dot_general(
            paired,
            weight_z,
            (((1,), (1,)), ((), ())),
            precision=exact_precision,
            preferred_element_type=jnp.float32,
        )
        return (totals + product, None)

    totals, unused = lax.scan(
        spread_step, jnp.zeros((slab_cells * column, grid_cells), jnp.float32), batches
    )
    return totals


def forward_lines(cos_tab, sin_tab, real_part, imag_part):
    return (
        matmul(cos_tab, real_part) + matmul(sin_tab, imag_part),
        matmul(cos_tab, imag_part) - matmul(sin_tab, real_part),
    )


def inverse_lines(cos_tab, sin_tab, real_part, imag_part):
    return (
        matmul(cos_tab, real_part) - matmul(sin_tab, imag_part),
        matmul(cos_tab, imag_part) + matmul(sin_tab, real_part),
    )


def on_device(atoms, pair_home, pair_other):
    grid_cells = NG
    groups = lax.axis_size("grp")
    domains = lax.axis_size("dom")
    pencils = lax.axis_size("pen")
    slab_cells = grid_cells // domains
    column = grid_cells // pencils
    atom_count = atoms.shape[3]
    tile_count = atom_count // TILE
    dom_at = lax.axis_index("dom")
    pen_at = lax.axis_index("pen")
    grp_at = lax.axis_index("grp")
    first_x = dom_at * slab_cells
    first_y = pen_at * column
    local_atoms = atoms.reshape(1, 1, 4 * atom_count)
    nearby = with_halo(local_atoms, (("dom", 0), ("pen", 1)), 1)
    nearby = nearby.reshape(3, 3, 4, atom_count)
    tiled = (
        nearby.reshape(9, 4, tile_count, TILE)
        .transpose(0, 2, 1, 3)
        .reshape(9 * tile_count, 4, TILE)
    )
    own_tiles = tiled[4 * tile_count : 5 * tile_count]
    home_ids = pair_home.reshape(-1)
    other_ids = pair_other.reshape(-1)
    pair_count = home_ids.shape[0]
    scales = jnp.array([2.0 * domains, 2.0 * pencils, 2.0 * domains], jnp.float32)

    def pair_group(id_pair):
        home_blk, other_blk = id_pair
        return pair_push(own_tiles[home_blk], tiled[other_blk], scales)

    pushes = lax.map(pair_group, (home_ids.reshape(-1, 16), other_ids.reshape(-1, 16)))
    pushes = pushes.reshape(pair_count, 3 * TILE)
    owners = (home_ids[:, None] == lax.broadcasted_iota(jnp.int32, (1, tile_count), 1)).astype(
        jnp.float32
    )
    summed = lax.dot_general(
        owners,
        pushes,
        (((0,), (0,)), ((), ())),
        precision=exact_precision,
        preferred_element_type=jnp.float32,
    )
    short_out = summed.reshape(tile_count, 3, TILE).transpose(1, 0, 2).reshape(3, 1, 1, atom_count)
    short_out = short_out * (2.0 / math.sqrt(atom_count / domains))
    spread_atoms = nearby[1:3, 1:3].transpose(2, 0, 1, 3).reshape(4, 4 * atom_count)
    z_ids = lax.iota(jnp.int32, grid_cells)
    cos_z, sin_z = phase_tables(z_ids, z_ids, grid_cells)
    charge_mesh = spread_mesh(spread_atoms, first_x, first_y, slab_cells, column, grid_cells)
    kz_rows = grid_cells // groups
    kz_part = kz_rows // domains
    kx_part = grid_cells // pencils
    z_real = matmul(charge_mesh, cos_z)
    z_imag = -matmul(charge_mesh, sin_z)
    sum_real, sum_imag = in_one_piece((z_real, z_imag), "grp", 1, 0)
    sum_real = sum_real.reshape(slab_cells, column, kz_rows)
    sum_imag = sum_imag.reshape(slab_cells, column, kz_rows)
    line_real, line_imag = side_by_side((sum_real, sum_imag), "dom", 2, 0, 1)
    fx_real, fx_imag = forward_lines(
        cos_z,
        sin_z,
        line_real.reshape(grid_cells, column * kz_part),
        line_imag.reshape(grid_cells, column * kz_part),
    )
    fx_real = fx_real.reshape(grid_cells, column, kz_part)
    fx_imag = fx_imag.reshape(grid_cells, column, kz_part)
    ylin_real, ylin_imag = side_by_side((fx_real, fx_imag), "pen", 0, 1, 2)
    ylin_real = ylin_real.transpose(1, 0, 2).reshape(grid_cells, kx_part * kz_part)
    ylin_imag = ylin_imag.transpose(1, 0, 2).reshape(grid_cells, kx_part * kz_part)
    fy_real, fy_imag = forward_lines(cos_z, sin_z, ylin_real, ylin_imag)
    kx_ids = pen_at * kx_part + lax.iota(jnp.int32, kx_part)
    kz_ids = grp_at * kz_rows + dom_at * kz_part + lax.iota(jnp.int32, kz_part)
    factor = green_factor(
        kx_ids[None, :, None], z_ids[:, None, None], kz_ids[None, None, :], grid_cells
    )
    factor = factor.reshape(grid_cells, kx_part * kz_part)
    iy_real, iy_imag = inverse_lines(cos_z, sin_z, fy_real * factor, fy_imag * factor)
    iy_real = iy_real.reshape(grid_cells, kx_part, kz_part).transpose(1, 0, 2)
    iy_imag = iy_imag.reshape(grid_cells, kx_part, kz_part).transpose(1, 0, 2)
    back_real, back_imag = side_by_side((iy_real, iy_imag), "pen", 1, 0, 2)
    ix_real, ix_imag = inverse_lines(
        cos_z,
        sin_z,
        back_real.reshape(grid_cells, column * kz_part),
        back_imag.reshape(grid_cells, column * kz_part),
    )
    ix_real = ix_real.reshape(grid_cells, column, kz_part)
    ix_imag = ix_imag.reshape(grid_cells, column, kz_part)
    slab_real, slab_imag = side_by_side((ix_real, ix_imag), "dom", 0, 2, 1)
    whole_real, whole_imag = rows_first((slab_real, slab_imag), "grp", (2, 2))
    own_pot = matmul(whole_real.reshape(-1, grid_cells), cos_z) - matmul(
        whole_imag.reshape(-1, grid_cells), sin_z
    )
    own_pot = own_pot.reshape(slab_cells, column, grid_cells)
    lower_planes = passed_along(own_pot[slab_cells - 3 :], "dom", 1)
    taller = jnp.concatenate([lower_planes, own_pot], axis=0)
    side_planes = passed_along(taller[:, column - 3 :], "pen", 1)
    rimmed = jnp.concatenate([side_planes, taller], axis=1)
    flat_pot = rimmed.transpose(1, 0, 2).reshape(-1, grid_cells)
    batch_size = min(256, atom_count)
    own_atoms = atoms.reshape(4, -1, batch_size).transpose(1, 0, 2)

    def interpolate(atom_batch):
        weight_x, slope_x = spline_rows(atom_batch[0], first_x - 3, slab_cells + 3, grid_cells)
        weight_y, slope_y = spline_rows(atom_batch[1], first_y - 3, column + 3, grid_cells)
        weight_z, slope_zw = spline_rows(atom_batch[2], 0, grid_cells, grid_cells)
        along_z = matmul(flat_pot, weight_z).reshape(column + 3, slab_cells + 3, batch_size)
        slope_z = matmul(flat_pot, slope_zw).reshape(column + 3, slab_cells + 3, batch_size)
        grad_x = jnp.sum(weight_y[:, None] * slope_x[None] * along_z, axis=(0, 1))
        grad_y = jnp.sum(slope_y[:, None] * weight_x[None] * along_z, axis=(0, 1))
        grad_z = jnp.sum(weight_y[:, None] * weight_x[None] * slope_z, axis=(0, 1))
        return jnp.stack([grad_x, grad_y, grad_z]) * atom_batch[3][None, :]

    gradients = lax.map(interpolate, own_atoms)
    gradients = gradients.transpose(1, 0, 2).reshape(3, 1, 1, atom_count)
    total_atoms = atom_count * groups * domains * pencils
    long_scale = -0.4 * grid_cells / math.sqrt(grid_cells * total_atoms)
    return (short_out, gradients * long_scale)


def solution(mesh):
    placed = (P(None, "grp", "dom", "pen"), P("grp", "dom", "pen"), P("grp", "dom", "pen"))
    return jax.shard_map(
        on_device,
        mesh=mesh,
        in_specs=placed,
        out_specs=(P(None, "grp", "dom", "pen"), P(None, "grp", "dom", "pen")),
        check_vma=False,
    )
```

profile of v0, /device:TPU:1, one launch (start us, length us, event | category | flops | bytes accessed | tf_op | source)
XLA Modules:
  0.0 256.1 jit_solution(4375133805574292460)
XLA Ops:
  0.6 5.4 %collective-permute-start = (f32[1,1,16384]{2,1,0:T(1,128)}, f32[1,1,16384]{2,1,0:T(1,128)S(1)}, u32[]{:S(2)}, u32[]{:S(2)}) collective-permute-start(f32[1,1,16384]{2,1,0:T(1,128)} %bitcast.279), channel_id=1, source_target_pairs={{0,16},{16,32},{32,48},{48,64},{64,80},{80,96},{96,112},{112,128},... | collective-permute-start | bytes 196616 | tf_op jit(solution)/shard_map/ppermute | solution.py:21
  6.0 12.6 %collective-permute-start.1 = (f32[1,1,16384]{2,1,0:T(1,128)}, f32[1,1,16384]{2,1,0:T(1,128)S(1)}, u32[]{:S(2)}, u32[]{:S(2)}) collective-permute-start(f32[1,1,16384]{2,1,0:T(1,128)} %bitcast.280), channel_id=1, source_target_pairs={{16,0},{32,16},{48,32},{64,48},{80,64},{96,80},{112,96},{128,112},... | collective-permute-start | bytes 196616 | tf_op jit(solution)/shard_map/ppermute | solution.py:24
  18.7 1.0 collective-permute-done.1
  20.7 1.9 collective-permute-start.2
  22.6 14.2 %collective-permute-start.3 = (f32[3,1,16384]{2,1,0:T(1,128)S(1)}, f32[3,1,16384]{2,1,0:T(1,128)S(1)}, u32[]{:S(2)}, u32[]{:S(2)}) collective-permute-start(f32[3,1,16384]{2,1,0:T(1,128)S(1)} %pad_maximum_fusion.2), channel_id=1, source_target_pairs={{1,0},{2,1},{3,2},{4,3},{5,4},{6,5},{7,6},{8,7},{9,8},{10,9},{11,1... | collective-permute-start | bytes 589832 | tf_op jit(solution)/shard_map/ppermute | solution.py:24
  36.9 1.9 collective-permute-done.2
  39.4 1.4 pad_maximum_fusion
  41.4 17.0 %while.44 = (s32[]{:T(128)}, f32[64,128]{1,0:T(8,128)S(1)}, f32[16,4,1024]{2,1,0:T(4,128)S(1)}, s32[]{:T(128)}, s32[]{:T(128)}, /*index=5*/s32[]{:T(128)}, s32[]{:T(128)}, s32[]{}, s32[]{}, s32[]{}) while((s32[]{:T(128)}, f32[64,128]{1,0:T(8,128)S(1)}, f32[16,4,1024]{2,1,0:T(4,128)S(1)}, s32[]{:T(128)}, s32[]{:T(128)}, ...), condition=%wide.region_5.6_spmd.clone, body=%wide.region_4.5_spmd.clone.sunk | while | flops 102601736 | bytes 454827 | solution.py:178
  60.0 3.3 %all-to-all-start = ((f32[4,128,32]{1,2,0:T(8,128)}), f32[4,128,32]{1,2,0:T(8,128)S(1)}, u32[]{:S(2)}, u32[]{:S(2)}) async-start(f32[4,128,32]{1,2,0:T(8,128)} %bitcast.23), calls=%async_computation | async-start | bytes 131072 | tf_op jit(solution)/shard_map/all_to_all | solution.py:36
  63.5 4.3 %all-to-all-done = f32[4,128,32]{1,2,0:T(8,128)S(1)} async-done(((f32[4,128,32]{1,2,0:T(8,128)}), f32[4,128,32]{1,2,0:T(8,128)S(1)}, u32[]{:S(2)}, u32[]{:S(2)}) %all-to-all-start) | async-done | bytes 65568 | tf_op jit(solution)/shard_map/all_to_all | solution.py:36
  68.9 26.7 %all-to-all-start.1 = ((f32[16,1,256]{2,1,0:T(1,128)}), f32[16,1,256]{2,1,0:T(1,128)S(1)}, u32[]{:S(2)}, u32[]{:S(2)}) async-start(f32[16,1,256]{2,1,0:T(1,128)} %reshape.2148), calls=%async_computation.1 | async-start | bytes 32768 | tf_op jit(solution)/shard_map/all_to_all | solution.py:57
  95.8 9.6 %all-to-all-done.1 = f32[16,1,256]{2,1,0:T(1,128)S(1)} async-done(((f32[16,1,256]{2,1,0:T(1,128)}), f32[16,1,256]{2,1,0:T(1,128)S(1)}, u32[]{:S(2)}, u32[]{:S(2)}) %all-to-all-start.1) | async-done | bytes 16416 | tf_op jit(solution)/shard_map/all_to_all | solution.py:57
  110.2 14.4 %all-to-all-start.2 = ((f32[16,1,256]{2,1,0:T(1,128)}), f32[16,1,256]{2,1,0:T(1,128)S(1)}, u32[]{:S(2)}, u32[]{:S(2)}) async-start(f32[16,1,256]{2,1,0:T(1,128)} %reshape.2150), calls=%async_computation.2 | async-start | bytes 32768 | tf_op jit(solution)/shard_map/all_to_all | solution.py:57
  124.7 16.0 %all-to-all-done.2 = f32[16,1,256]{2,1,0:T(1,128)S(1)} async-done(((f32[16,1,256]{2,1,0:T(1,128)}), f32[16,1,256]{2,1,0:T(1,128)S(1)}, u32[]{:S(2)}, u32[]{:S(2)}) %all-to-all-start.2) | async-done | bytes 16416 | tf_op jit(solution)/shard_map/all_to_all | solution.py:57
  146.9 3.7 %all-to-all-start.3 = ((f32[16,1,256]{2,1,0:T(1,128)}), f32[16,1,256]{2,1,0:T(1,128)S(1)}, u32[]{:S(2)}, u32[]{:S(2)}) async-start(f32[16,1,256]{2,1,0:T(1,128)} %reshape.2152), calls=%async_computation.3 | async-start | bytes 32768 | tf_op jit(solution)/shard_map/all_to_all | solution.py:57
  153.3 13.1 %all-to-all-done.3 = f32[16,1,256]{2,1,0:T(1,128)S(1)} async-done(((f32[16,1,256]{2,1,0:T(1,128)}), f32[16,1,256]{2,1,0:T(1,128)S(1)}, u32[]{:S(2)}, u32[]{:S(2)}) %all-to-all-start.3) | async-done | bytes 16416 | tf_op jit(solution)/shard_map/all_to_all | solution.py:57
  171.0 6.6 %all-to-all-start.4 = ((f32[16,1,256]{2,1,0:T(1,128)}), f32[16,1,256]{2,1,0:T(1,128)S(1)}, u32[]{:S(2)}, u32[]{:S(2)}) async-start(f32[16,1,256]{2,1,0:T(1,128)} %reshape.2154), calls=%async_computation.4 | async-start | bytes 32768 | tf_op jit(solution)/shard_map/all_to_all | solution.py:57
  178.1 9.3 %all-to-all-done.4 = f32[16,1,256]{2,1,0:T(1,128)S(1)} async-done(((f32[16,1,256]{2,1,0:T(1,128)}), f32[16,1,256]{2,1,0:T(1,128)S(1)}, u32[]{:S(2)}, u32[]{:S(2)}) %all-to-all-start.4) | async-done | bytes 16416 | tf_op jit(solution)/shard_map/all_to_all | solution.py:57
  189.0 9.0 %all_gather.3 = f32[128,128]{1,0:T(8,128)S(1)} all-gather(f32[32,128]{1,0:T(8,128)S(1)} %pad_maximum_fusion.8), channel_id=1, replica_groups=mesh['grp'=4,'dom'=16,'pen'=16] {'grp'}, dimensions={0}, use_global_device_ids=true | all-gather | bytes 81920 | tf_op jit(solution)/shard_map/all_gather | solution.py:68
  199.1 5.6 %collective-permute-start.4 = (f32[3,8,128]{2,1,0:T(8,128)S(1)}, f32[3,8,128]{2,1,0:T(8,128)S(1)}, u32[]{:S(2)}, u32[]{:S(2)}) collective-permute-start(f32[3,8,128]{2,1,0:T(8,128)S(1)} %slice_bitcast_fusion.3), channel_id=1, source_target_pairs={{240,0},{0,16},{16,32},{32,48},{48,64},{64,80},{80,96},{96,112},{1... | collective-permute-start | bytes 36872 | tf_op jit(solution)/shard_map/ppermute | solution.py:81
  204.7 17.9 %while.43 = (s32[]{:T(128)}, f32[4,16,3,128]{3,2,1,0:T(4,128)S(1)}, s32[4,16]{1,0:T(4,128)S(1)}, f32[32,4,128]{2,1,0:T(4,128)S(1)}, s32[4,16]{1,0:T(4,128)S(1)}, /*index=5*/f32[288,4,128]{2,1,0:T(4,128)S(1)}, s32[]{:T(128)}) while((s32[]{:T(128)}, f32[4,16,3,128]{3,2,1,0:T(4,128)S(1)}, s32[4,16]{1,0:T(4,128)S(1)}, ...), condition=%wide.region_3.4_spmd.clone, body=%wide.region_0.3_spmd.sunk.clone.sunk | while | flops 10750050 | bytes 4571733 | solution.py:230
  206.0 1.1 fusion.309
  207.3 1.9 fusion.310
  210.4 1.1 fusion.309
  211.8 1.9 fusion.310
  214.9 1.1 fusion.309
  216.3 1.9 fusion.310
  219.4 1.1 fusion.309
  220.8 1.9 fusion.310
  222.7 2.2 collective-permute-start.5
  225.7 12.3 %collective-permute-done.5 = f32[11,3,128]{2,1,0:T(4,128)S(1)} collective-permute-done((f32[11,3,128]{2,1,0:T(4,128)S(1)}, f32[11,3,128]{2,1,0:T(4,128)S(1)}, u32[]{:S(2)}, u32[]{:S(2)}) %collective-permute-start.5) | collective-permute-done | bytes 16928 | tf_op jit(solution)/shard_map/ppermute | solution.py:81
  238.1 17.2 %while.42 = (s32[]{:T(128)}, f32[16,3,256]{2,1,0:T(4,128)S(1)}, f32[16,4,256]{2,0,1:T(8,128)S(1)}, s32[]{:T(128)}, s32[]{:T(128)}, /*index=5*/f32[121,128]{1,0:T...) while((s32[]{:T(128)}, f32[16,3,256]{2,1,0:T(4,128)S(1)}, f32[16,4,256]{2,0,1:T(8,128)S(1)}, ...), condition=%wide.region_11.12_spmd, body=%wide.region_7.11_spmd.sunk | while | flops 96324352 | bytes 1804465 | solution.py:312
  (561 shorter events, 65.2 us)
Async XLA Ops:
  0.6 18.0 %collective-permute-start = (f32[1,1,16384]{2,1,0:T(1,128)}, f32[1,1,16384]{2,1,0:T(1,128)S(1)}, u32[]{:S(2)}, u32[]{:S(2)}) collective-permute-start(f32[1,1,16384]{2,1,0:T(1,128)} %bitcast.279), channel_id=1, source_target_pairs={{0,16},{16,32},{32,48},{48,64},{64,80},{80,96},{96,112},{112,128},... | collective-permute-start | bytes 196616 | tf_op jit(solution)/shard_map/ppermute | solution.py:21
  6.0 13.7 %collective-permute-start.1 = (f32[1,1,16384]{2,1,0:T(1,128)}, f32[1,1,16384]{2,1,0:T(1,128)S(1)}, u32[]{:S(2)}, u32[]{:S(2)}) collective-permute-start(f32[1,1,16384]{2,1,0:T(1,128)} %bitcast.280), channel_id=1, source_target_pairs={{16,0},{32,16},{48,32},{64,48},{80,64},{96,80},{112,96},{128,112},... | collective-permute-start | bytes 196616 | tf_op jit(solution)/shard_map/ppermute | solution.py:24
  20.7 18.1 %collective-permute-start.2 = (f32[3,1,16384]{2,1,0:T(1,128)S(1)}, f32[3,1,16384]{2,1,0:T(1,128)S(1)}, u32[]{:S(2)}, u32[]{:S(2)}) collective-permute-start(f32[3,1,16384]{2,1,0:T(1,128)S(1)} %pad_maximum_fusion.2), channel_id=1, source_target_pairs={{0,1},{1,2},{2,3},{3,4},{4,5},{5,6},{6,7},{7,8},{8,9},{9,10},{10,1... | collective-permute-start | bytes 589832 | tf_op jit(solution)/shard_map/ppermute | solution.py:21
  22.6 16.8 %collective-permute-start.3 = (f32[3,1,16384]{2,1,0:T(1,128)S(1)}, f32[3,1,16384]{2,1,0:T(1,128)S(1)}, u32[]{:S(2)}, u32[]{:S(2)}) collective-permute-start(f32[3,1,16384]{2,1,0:T(1,128)S(1)} %pad_maximum_fusion.2), channel_id=1, source_target_pairs={{1,0},{2,1},{3,2},{4,3},{5,4},{6,5},{7,6},{8,7},{9,8},{10,9},{11,1... | collective-permute-start | bytes 589832 | tf_op jit(solution)/shard_map/ppermute | solution.py:24
  60.0 7.8 %all-to-all-start = ((f32[4,128,32]{1,2,0:T(8,128)}), f32[4,128,32]{1,2,0:T(8,128)S(1)}, u32[]{:S(2)}, u32[]{:S(2)}) async-start(f32[4,128,32]{1,2,0:T(8,128)} %bitcast.23), calls=%async_computation | async-start | bytes 131072 | tf_op jit(solution)/shard_map/all_to_all | solution.py:36
  68.9 36.4 %all-to-all-start.1 = ((f32[16,1,256]{2,1,0:T(1,128)}), f32[16,1,256]{2,1,0:T(1,128)S(1)}, u32[]{:S(2)}, u32[]{:S(2)}) async-start(f32[16,1,256]{2,1,0:T(1,128)} %reshape.2148), calls=%async_computation.1 | async-start | bytes 32768 | tf_op jit(solution)/shard_map/all_to_all | solution.py:57
  110.2 30.5 %all-to-all-start.2 = ((f32[16,1,256]{2,1,0:T(1,128)}), f32[16,1,256]{2,1,0:T(1,128)S(1)}, u32[]{:S(2)}, u32[]{:S(2)}) async-start(f32[16,1,256]{2,1,0:T(1,128)} %reshape.2150), calls=%async_computation.2 | async-start | bytes 32768 | tf_op jit(solution)/shard_map/all_to_all | solution.py:57
  143.5 7.1 %copy-start = (f32[4,1,1,4096]{3,2,1,0:T(1,128)S(1)}, f32[4,1,1,4096]{3,2,1,0:T(1,128)}, u32[]{:S(2)}) copy-start(f32[4,1,1,4096]{3,2,1,0:T(1,128)} %param.10) | copy-start | bytes 196612
  143.9 7.4 %copy-start.1 = (s32[1,1,64]{2,1,0:T(1,128)S(1)}, s32[1,1,64]{2,1,0:T(1,128)}, u32[]{:S(2)}) copy-start(s32[1,1,64]{2,1,0:T(1,128)} %param.11) | copy-start | bytes 772
  143.9 8.1 %copy-start.2 = (s32[1,1,64]{2,1,0:T(1,128)S(1)}, s32[1,1,64]{2,1,0:T(1,128)}, u32[]{:S(2)}) copy-start(s32[1,1,64]{2,1,0:T(1,128)} %param.12) | copy-start | bytes 772
  146.9 19.5 %all-to-all-start.3 = ((f32[16,1,256]{2,1,0:T(1,128)}), f32[16,1,256]{2,1,0:T(1,128)S(1)}, u32[]{:S(2)}, u32[]{:S(2)}) async-start(f32[16,1,256]{2,1,0:T(1,128)} %reshape.2152), calls=%async_computation.3 | async-start | bytes 32768 | tf_op jit(solution)/shard_map/all_to_all | solution.py:57
  171.0 16.5 %all-to-all-start.4 = ((f32[16,1,256]{2,1,0:T(1,128)}), f32[16,1,256]{2,1,0:T(1,128)S(1)}, u32[]{:S(2)}, u32[]{:S(2)}) async-start(f32[16,1,256]{2,1,0:T(1,128)} %reshape.2154), calls=%async_computation.4 | async-start | bytes 32768 | tf_op jit(solution)/shard_map/all_to_all | solution.py:57
  199.1 23.5 %collective-permute-start.4 = (f32[3,8,128]{2,1,0:T(8,128)S(1)}, f32[3,8,128]{2,1,0:T(8,128)S(1)}, u32[]{:S(2)}, u32[]{:S(2)}) collective-permute-start(f32[3,8,128]{2,1,0:T(8,128)S(1)} %slice_bitcast_fusion.3), channel_id=1, source_target_pairs={{240,0},{0,16},{16,32},{32,48},{48,64},{64,80},{80,96},{96,112},{1... | collective-permute-start | bytes 36872 | tf_op jit(solution)/shard_map/ppermute | solution.py:81
  222.7 15.4 %collective-permute-start.5 = (f32[11,3,128]{2,1,0:T(4,128)S(1)}, f32[11,3,128]{2,1,0:T(4,128)S(1)}, u32[]{:S(2)}, u32[]{:S(2)}) collective-permute-start(f32[11,3,128]{2,1,0:T(4,128)S(1)} %pad_maximum_fusion.6), channel_id=1, source_target_pairs={{15,0},{0,1},{1,2},{2,3},{3,4},{4,5},{5,6},{6,7},{7,8},{8,9},{9,10... | collective-permute-start | bytes 50696 | tf_op jit(solution)/shard_map/ppermute | solution.py:81
where the time goes:
time: 257 us; the launch traced here: 256 us
  starting transfers between devices  96.6 us (38%)
  waiting for transfers between devices  68.2 us (27%)
  matrix products  33.6 us (13%)
  other arithmetic  26.4 us (10%)
  local copies, waits for them, and re-layouts  17.8 us (7%)
  blocking collectives  8.97 us (3%)
  loops' own time  3.19 us (1%)
    all_to_all x4, starting transfers between devices, side_by_side(): lax.all_to_all(both, axis, split_axis=split_dim, concat_axis=concat_dim,...  51.4 us
    all_to_all x4, waiting for transfers between devices, side_by_side(): lax.all_to_all(both, axis, split_axis=split_dim, concat_axis=concat_dim,...  48 us
    ppermute x2, starting transfers between devices, with_halo(): lax.ppermute(lax.slice_in_dim(block, 0, width, axis=dim), axis, backward)  26.8 us
    dot_general x52, matrix products, matmul(): jnp.dot(left, right, precision=exact_precision, preferred_element_type=jn...  19.5 us
    dot_general x16, matrix products, spread_step(): lax.dot_general(paired, weight_z, (((1,), (1,)), ((), ())), precision=exa...  13.3 us
    ppermute x2, waiting for transfers between devices, passed_along(): return lax.ppermute(block, axis, route)  12.3 us
    all_gather x1, blocking collectives, rows_first(): filled = lax.all_gather(both, axis, axis=0, tiled=True)  8.97 us
    ppermute x2, starting transfers between devices, passed_along(): return lax.ppermute(block, axis, route)  7.83 us
  transfers between devices with their start and end apart: 11, of which 9 were waited for; matrix products, arithmetic and copies ran while one was open for 9% of the time, Pallas kernels for 0%

commit v1 on v0

v1 whole, which is shorter than its diff:
```python
import functools
import math

import jax
import jax.numpy as jnp
import numpy as np
from jax import lax
from jax.experimental import pallas as pl
from jax.experimental.pallas import tpu as pltpu
from jax.sharding import PartitionSpec as P

NG = 128
TILE = 128
TILES = 32
PAIRS = 64
SIDE = 11
PEERS = 32
MESH = pl.DeviceIdType.MESH
f32 = jnp.float32
bf16 = jnp.bfloat16


def basis(cells):
    k = np.arange(NG)[:, None]
    m = np.where(k <= NG // 2, k, k - NG // 2)
    angle = 2.0 * np.pi * np.mod(m * cells[None, :], NG) / NG
    return np.where(k <= NG // 2, np.cos(angle), np.sin(angle))


def turning(starts, lanes, used):
    k = np.arange(NG)[:, None]
    m = np.where(k <= NG // 2, k, k - NG // 2)
    first = 2.0 * np.pi * np.mod(m * starts[None, :], NG) / NG
    second = 2.0 * np.pi * np.mod(m * lanes[None, :], NG) / NG
    is_cos = k <= NG // 2
    part_c = np.where(is_cos, np.cos(second), np.sin(second)) * used[None, :]
    part_s = np.where(is_cos, -np.sin(second), np.cos(second)) * used[None, :]
    return np.cos(first), np.sin(first), part_c, part_s


def halves(table):
    table = np.asarray(table, np.float32)
    high = table.astype(jnp.bfloat16)
    low = (table - high.astype(np.float32)).astype(jnp.bfloat16)
    return high, low


def spread_columns(turn_c, turn_s, inner):
    count = turn_c.shape[1]
    out = np.zeros((inner, 2, NG, count, inner))
    for i in range(inner):
        out[i, 0, :, :, i] = turn_c
        out[i, 1, :, :, i] = turn_s
    return out.reshape(inner * 2 * NG, count * inner)


def make_tables():
    row = np.arange(NG)
    row_x, row_y = row // SIDE, row % SIDE
    lane_z, lane_y = (row // 16) % 2, row % 16
    x_c, x_s, bx_c, bx_s = turning(8 * np.arange(16), row_x - 3, row < SIDE * SIDE)
    y_c, y_s, by_c, by_s = turning(8 * np.arange(8), 64 * lane_z - 3 + lane_y, lane_y < SIDE)
    x_cols, y_cols = spread_columns(x_c, x_s, 4), spread_columns(y_c, y_s, 4)
    xh, xl = halves(x_cols)
    yh, yl = halves(y_cols)
    forward_x = np.concatenate([xh, xh, xl], axis=1)
    forward_y = np.concatenate([yh, yh, yl], axis=1)
    inverse_x = np.concatenate([xh.T, xl.T], axis=0)
    inverse_y = np.concatenate([yh.T, yl.T], axis=0)
    pick_x = np.zeros((4, 2, NG, NG), np.float32)
    for j in range(4):
        for z in range(2):
            for r in range(SIDE * SIDE):
                pick_x[j, z, r, j * 32 + z * 16 + row_y[r]] = 1.0
    pick_y = np.zeros((4, NG, NG), np.float32)
    for i in range(4):
        for lane in range(NG):
            pick_y[i, lane, i * 4 + lane // 32] = 1.0
    zh, zl = halves(basis(row))
    return dict(
        basis_z=np.concatenate([zh, zl], axis=0),
        forward_x=forward_x,
        forward_y=forward_y,
        inverse_x=inverse_x,
        inverse_y=inverse_y,
        pick_x=pick_x.reshape(1024, NG).astype(jnp.bfloat16),
        pick_y=pick_y.reshape(512, NG).astype(jnp.bfloat16),
        parts=np.concatenate([bx_c, bx_s, by_c, by_s], axis=0).astype(np.float32),
    )


NAMES = (
    "basis_z",
    "forward_x",
    "forward_y",
    "inverse_x",
    "inverse_y",
    "pick_x",
    "pick_y",
    "parts",
)


def dot(a, b):
    return lax.dot_general(a, b, (((1,), (0,)), ((), ())), preferred_element_type=f32)


def dot_nt(a, b):
    return lax.dot_general(a, b, (((1,), (1,)), ((), ())), preferred_element_type=f32)


def split(x):
    high = x.astype(bf16)
    return high, (x - high.astype(f32)).astype(bf16)


def stacked(x):
    high = x.astype(bf16).astype(f32)
    return jnp.concatenate([high, x - high, high], axis=0).astype(bf16)


def spline_terms(scaled):
    floored = jnp.floor(scaled)
    w = scaled - floored
    remain = 1.0 - w
    sq = w * w
    cube = sq * w
    thetas = [
        remain * remain * remain * (1.0 / 6.0),
        (3.0 * cube - 6.0 * sq + 4.0) * (1.0 / 6.0),
        (-3.0 * cube + 3.0 * sq + 3.0 * w + 1.0) * (1.0 / 6.0),
        cube * (1.0 / 6.0),
    ]
    slopes = [
        -0.5 * remain * remain,
        1.5 * sq - 2.0 * w,
        -1.5 * sq + w + 0.5,
        0.5 * sq,
    ]
    return floored, thetas, slopes


def one_of(is_at, values):
    out = jnp.where(is_at[3], values[3], 0.0)
    for k in (2, 1, 0):
        out = jnp.where(is_at[k], values[k], out)
    return out


def matches(t):
    return [t == k for k in range(4)]


def to_lines_x(got, forward_x, part_c, part_s, pick_x):
    both = jnp.concatenate([got[:64], got[64:]], axis=1)
    turned = dot(forward_x, stacked(both))
    c2, s2 = jnp.concatenate([part_c] * 2, axis=1), jnp.concatenate([part_s] * 2, axis=1)
    out = None
    for j in range(4):
        q = c2 * turned[j * 256 : j * 256 + 128] + s2 * turned[j * 256 + 128 : j * 256 + 256]
        high, low = split(q)
        pick = pick_x[j * 256 : (j + 1) * 256]
        term = dot(high, pick) + dot(low, pick)
        out = term if out is None else out + term
    return out


def through_y(got, factor, forward_y, inverse_y, part_c, part_s, pick_y):
    total = (got[:32] + got[32:64]) + (got[64:96] + got[96:])
    turned = dot(forward_y, stacked(total))
    lines = jnp.concatenate(
        [
            part_c * turned[i * 256 : i * 256 + 128] + part_s * turned[i * 256 + 128 : i * 256 + 256]
            for i in range(4)
        ],
        axis=1,
    )
    high, low = split(lines)
    freq = (dot(high, pick_y) + dot(low, pick_y)) * factor
    high, low = split(freq)
    wide = dot_nt(high, pick_y) + dot_nt(low, pick_y)
    out = None
    for i in range(4):
        piece = wide[:, i * 128 : (i + 1) * 128]
        high, low = split(jnp.concatenate([part_c * piece, part_s * piece], axis=0))
        table = inverse_y[:, i * 256 : (i + 1) * 256]
        full = dot(table, high)
        term = full[:32] + full[32:] + dot(table[:32], low)
        out = term if out is None else out + term
    return out


def from_lines_x(got, inverse_x, part_c, part_s, pick_x):
    high, low = split(got)
    c2, s2 = jnp.concatenate([part_c] * 2, axis=1), jnp.concatenate([part_s] * 2, axis=1)
    out = None
    for j in range(4):
        pick = pick_x[j * 256 : (j + 1) * 256]
        wide = dot_nt(high, pick) + dot_nt(low, pick)
        q_high, q_low = split(jnp.concatenate([c2 * wide, s2 * wide], axis=0))
        table = inverse_x[:, j * 256 : (j + 1) * 256]
        full = dot(table, q_high)
        term = full[:64] + full[64:] + dot(table[:64], q_low)
        out = term if out is None else out + term
    return jnp.concatenate([out[:, :128], out[:, 128:]], axis=0)


def to_z(mesh, basis_z):
    high, low = split(mesh)
    full = dot(basis_z, high)
    return full[:128] + full[128:] + dot(basis_z[:128], low)


def from_z(got, basis_z):
    high, low = split(got.T)
    return dot(high, basis_z[:128]) + dot(high, basis_z[128:]) + dot(low, basis_z[:128])


def green_of(k_x, k_y, k_z):
    def mode(k):
        return jnp.where(k <= NG // 2, k, k - NG // 2)

    def weight(m):
        ratio = (2.0 + jnp.cos(m.astype(f32) * (2.0 * math.pi / NG))) / 3.0
        twice = jnp.where((m == 0) | (m == NG // 2), 1.0, 2.0)
        return twice / (ratio * ratio)

    m_x, m_y, m_z = mode(k_x), mode(k_y), mode(k_z)
    square = (m_x * m_x + m_z * m_z + m_y * m_y).astype(f32)
    beta = 0.6 * NG
    value = jnp.exp(square * (-math.pi * math.pi / (beta * beta)))
    value = value / (math.pi * jnp.maximum(square, 1.0))
    value = value * (weight(m_x) * weight(m_z)) * weight(m_y)
    return jnp.where(square > 0.5, value, 0.0)


def pair_push(home, other, scales):
    scaled = []
    for c in range(3):
        delta = home[c] - other[:, c : c + 1]
        delta = delta - jnp.floor(delta + 0.5)
        scaled.append(delta * scales[c])
    square = scaled[0] * scaled[0] + scaled[1] * scaled[1] + scaled[2] * scaled[2]
    weight = jnp.exp(-0.5 * square) * other[:, 3:4]
    return [jnp.sum(s * weight, axis=0, keepdims=True) for s in scaled]


LOW = 0
THETA = 3
SLOPE = 15
CHARGED = 27
FIELDS = 31


def kernel(
    atoms_hbm,
    home_smem,
    other_smem,
    home_vmem,
    basis_hbm,
    fx_hbm,
    fy_hbm,
    ix_hbm,
    iy_hbm,
    px_hbm,
    py_hbm,
    parts_hbm,
    short_ref,
    long_ref,
    near,
    fields,
    mesh,
    pushes,
    grads,
    pot_parts,
    send_a,
    recv_a,
    send_b,
    recv_b,
    send_c,
    recv_c,
    send_d,
    recv_d,
    basis_z,
    forward_x,
    forward_y,
    inverse_x,
    inverse_y,
    pick_x,
    pick_y,
    parts,
    table_sems,
    atom_sem,
    send_sems,
    recv_sems,
    halo_send,
    halo_recv,
):
    grp = lax.axis_index("grp")
    dom = lax.axis_index("dom")
    pen = lax.axis_index("pen")
    z_hi, y_at = pen // 8, lax.rem(pen, 8)
    at_a = z_hi * 16 + dom
    at_b = grp * 8 + y_at

    def peer_a(k):
        t = lax.rem(at_a + k, PEERS)
        return t, {"grp": grp, "dom": lax.rem(t, 16), "pen": (t // 16) * 8 + y_at}

    def peer_b(k):
        b = lax.rem(at_b + k, PEERS)
        return b, {"grp": b // 8, "dom": dom, "pen": z_hi * 8 + lax.rem(b, 8)}

    pen_next = {"grp": grp, "dom": dom, "pen": lax.rem(pen + 1, 16)}
    pen_prev = {"grp": grp, "dom": dom, "pen": lax.rem(pen + 15, 16)}
    dom_next = {"grp": grp, "dom": lax.rem(dom + 1, 16), "pen": pen}
    dom_prev = {"grp": grp, "dom": lax.rem(dom + 15, 16), "pen": pen}

    load_atoms = pltpu.make_async_copy(atoms_hbm, near.at[4], atom_sem)
    load_atoms.start()
    barrier = pltpu.get_barrier_semaphore()

    def greet(k, carry):
        pl.semaphore_signal(barrier, 1, device_id=peer_a(k)[1], device_id_type=MESH)
        pl.semaphore_signal(barrier, 1, device_id=peer_b(k)[1], device_id_type=MESH)
        return carry

    lax.fori_loop(1, PEERS, greet, 0)
    pl.semaphore_signal(barrier, 1, device_id=pen_next, device_id_type=MESH)
    pl.semaphore_signal(barrier, 1, device_id=pen_prev, device_id_type=MESH)

    loads = [
        pltpu.make_async_copy(source, target, table_sems.at[n])
        for n, (source, target) in enumerate(
            (
                (basis_hbm, basis_z),
                (fx_hbm, forward_x),
                (fy_hbm, forward_y),
                (ix_hbm, inverse_x),
                (iy_hbm, inverse_y),
                (px_hbm, pick_x),
                (py_hbm, pick_y),
                (parts_hbm, parts),
            )
        )
    ]
    for load in loads:
        load.start()
    load_atoms.wait()

    charge = near[4, 3]
    for c, start in ((0, (dom * 8).astype(f32)), (1, (pen * 8).astype(f32)), (2, 3.0)):
        floored, thetas, slopes = spline_terms(near[4, c] * float(NG))
        fields[LOW + c] = floored - start
        for k in range(4):
            fields[THETA + 4 * c + k] = thetas[k]
            fields[SLOPE + 4 * c + k] = slopes[k]
            if c == 1:
                fields[CHARGED + k] = thetas[k] * charge

    column = lax.broadcasted_iota(jnp.int32, (NG, TILE), 0)
    patch_x = jnp.floor((column.astype(f32) + 0.5) * (1.0 / SIDE))
    patch_y = column.astype(f32) - SIDE * patch_x

    def row(field, tile):
        return fields[field, pl.ds(tile, 1), :]

    def at_z(tile):
        return matches((column - row(LOW + 2, tile).astype(jnp.int32)) & (NG - 1))

    mesh[...] = jnp.zeros_like(mesh)

    def spread(step, carry):
        z_parts, p_parts = [], []
        for n in range(4):
            tile = step * 4 + n
            w_z = one_of(at_z(tile), [row(THETA + 8 + k, tile) for k in range(4)])
            w_x = one_of(
                matches(patch_x - row(LOW, tile)), [row(THETA + k, tile) for k in range(4)]
            )
            w_y = one_of(
                matches(patch_y - row(LOW + 1, tile)), [row(CHARGED + k, tile) for k in range(4)]
            )
            z_parts.append(split(w_z))
            p_parts.append(split(w_x * w_y))
        z_high = jnp.concatenate([z[0] for z in z_parts], axis=1)
        z_low = jnp.concatenate([z[1] for z in z_parts], axis=1)
        p_high = jnp.concatenate([p[0] for p in p_parts], axis=1)
        p_low = jnp.concatenate([p[1] for p in p_parts], axis=1)
        wide = dot_nt(z_high, jnp.concatenate([p_high, p_low], axis=0))
        mesh[...] += wide[:, :128] + wide[:, 128:] + dot_nt(z_low, p_high)
        return carry

    lax.fori_loop(0, TILES // 4, spread, 0)

    def put(ref, value):
        for n in range(value.shape[0] // 4):
            ref[n] = value[4 * n : 4 * n + 4]

    def taken(ref):
        return jnp.concatenate([ref[n] for n in range(PEERS)], axis=0)

    def exchange(source, target, phase, peer, own, slot):
        def post(k, carry):
            index, device = peer(k)
            pltpu.make_async_remote_copy(
                src_ref=source.at[slot(index)],
                dst_ref=target.at[own],
                send_sem=send_sems.at[phase],
                recv_sem=recv_sems.at[phase],
                device_id=device,
                device_id_type=MESH,
            ).start()
            return carry

        lax.fori_loop(1, PEERS, post, 0)
        target[own] = source[slot(own)]

    def arrived(target, phase, device):
        whole = target.at[pl.ds(0, PEERS - 1)]
        both = pltpu.make_async_remote_copy(
            src_ref=whole,
            dst_ref=whole,
            send_sem=send_sems.at[phase],
            recv_sem=recv_sems.at[phase],
            device_id=device,
            device_id_type=MESH,
        )
        both.wait_recv()
        both.wait_send()

    def same(index):
        return index

    loads[0].wait()
    put(send_a, to_z(mesh[...], basis_z[...]))
    pl.semaphore_wait(barrier, 2 * (PEERS - 1) + 2)
    exchange(send_a, recv_a, 0, peer_a, at_a, same)

    def halo(source, target, n, device):
        return pltpu.make_async_remote_copy(
            src_ref=near.at[source],
            dst_ref=near.at[target],
            send_sem=halo_send.at[n],
            recv_sem=halo_recv.at[n],
            device_id=device,
            device_id_type=MESH,
        )

    side = [halo(4, 3, 0, pen_next), halo(4, 5, 1, pen_prev)]
    for copy in side:
        copy.start()

    for load in loads[1:]:
        load.wait()
    part_xc, part_xs, part_yc, part_ys = (parts[128 * n : 128 * n + 128, :] for n in range(4))
    lane = lax.broadcasted_iota(jnp.int32, (1, NG), 1)
    k_x = at_b * 4 + (lane // 4)
    k_z = at_a * 4 + lax.rem(lane, 4)
    k_y = lax.broadcasted_iota(jnp.int32, (NG, 1), 0)
    used = lane < 16
    factor = green_of(jnp.where(used, k_x, 1), k_y, jnp.where(used, k_z, 1))

    peer_one_a = peer_a(1)[1]
    peer_one_b = peer_b(1)[1]
    arrived(recv_a, 0, peer_one_a)
    put(send_b, to_lines_x(taken(recv_a), forward_x[...], part_xc, part_xs, pick_x[...]))
    exchange(send_b, recv_b, 1, peer_b, at_b, same)

    arrived(recv_b, 1, peer_one_b)
    put(
        send_c,
        through_y(
            taken(recv_b),
            factor,
            forward_y[...],
            inverse_y[...],
            part_yc,
            part_ys,
            pick_y[...],
        ),
    )
    exchange(send_c, recv_c, 2, peer_b, at_b, lambda index: lax.rem(index, 8))

    for copy in side:
        copy.wait()
    ends = [
        halo(pl.ds(3, 3), pl.ds(0, 3), 2, dom_next),
        halo(pl.ds(3, 3), pl.ds(6, 3), 3, dom_prev),
    ]
    for copy in ends:
        copy.start()

    arrived(recv_c, 2, peer_one_b)
    put(send_d, from_lines_x(taken(recv_c), inverse_x[...], part_xc, part_xs, pick_x[...]))
    exchange(send_d, recv_d, 3, peer_a, at_a, same)

    for copy in ends:
        copy.wait()
    scales = (32.0, 32.0, 32.0)
    pad = jnp.zeros((4, TILE), f32)

    def pair(n, carry):
        home, other = home_smem[n], other_smem[n]
        own = [near[4, c, pl.ds(home, 1), :] for c in range(3)]
        far = [near[other >> 5, c, pl.ds(other & 31, 1), :] for c in range(4)]
        rows = pair_push(own, jnp.concatenate(far + [pad], axis=0).T, scales)
        for c in range(3):
            pushes[c, pl.ds(n, 1), :] = rows[c]
        return carry

    lax.fori_loop(0, PAIRS, pair, 0, unroll=2)
    tile_ids = lax.broadcasted_iota(jnp.int32, (TILES, PAIRS), 0)
    owners = jnp.where(home_vmem[...] == tile_ids, 1.0, 0.0).astype(bf16)
    for c in range(3):
        high, low = split(pushes[c])
        short_ref[c] = (dot(owners, high) + dot(owners, low)) * (charge * (2.0 / math.sqrt(256.0)))

    arrived(recv_d, 3, peer_one_a)
    pot_high, pot_low = split(from_z(taken(recv_d), basis_z[...]))
    pot_parts[:128] = pot_high
    pot_parts[128:] = pot_low

    def interpolate(step, carry):
        for n in range(2):
            tile = step * 2 + n
            is_z = at_z(tile)
            w_z = one_of(is_z, [row(THETA + 8 + k, tile) for k in range(4)])
            s_z = one_of(is_z, [row(SLOPE + 8 + k, tile) for k in range(4)])
            high, low = split(jnp.concatenate([w_z, s_z], axis=1))
            full = dot(pot_parts[...], high)
            along = full[:128] + full[128:] + dot(pot_parts[:128], low)
            is_x = matches(patch_x - row(LOW, tile))
            w_x = one_of(is_x, [row(THETA + k, tile) for k in range(4)])
            s_x = one_of(is_x, [row(SLOPE + k, tile) for k in range(4)])
            is_y = matches(patch_y - row(LOW + 1, tile))
            w_y = one_of(is_y, [row(THETA + 4 + k, tile) for k in range(4)])
            s_y = one_of(is_y, [row(SLOPE + 4 + k, tile) for k in range(4)])
            value, slope = along[:, :128], along[:, 128:]
            sums = (s_x * (w_y * value), w_x * (s_y * value), w_x * (w_y * slope))
            for c in range(3):
                grads[c, pl.ds(tile, 1), :] = jnp.sum(sums[c], axis=0, keepdims=True)
        return carry

    lax.fori_loop(0, TILES // 2, interpolate, 0)
    total_atoms = 4 * 16 * 16 * 4096
    scale = -0.4 * NG / math.sqrt(NG * total_atoms)
    for c in range(3):
        long_ref[c] = grads[c] * (charge * scale)


def on_device(atoms, pair_home, pair_other, *tables):
    any_spec = pl.BlockSpec(memory_space=pl.ANY)
    smem = pl.BlockSpec(memory_space=pltpu.SMEM)
    vmem = pl.BlockSpec(memory_space=pltpu.VMEM)
    blocks = atoms.reshape(4, TILES, TILE)
    homes = pair_home.reshape(PAIRS)
    others = pair_other.reshape(PAIRS)
    force = jax.ShapeDtypeStruct((3, TILES, TILE), f32)
    message = pltpu.VMEM((PEERS, 4, NG), f32)
    short, long = pl.pallas_call(
        kernel,
        out_shape=(force, force),
        in_specs=[any_spec, smem, smem, vmem] + [any_spec] * len(NAMES),
        out_specs=(vmem, vmem),
        scratch_shapes=[
            pltpu.VMEM((9, 4, TILES, TILE), f32),
            pltpu.VMEM((FIELDS, TILES, TILE), f32),
            pltpu.VMEM((NG, NG), f32),
            pltpu.VMEM((3, PAIRS, TILE), f32),
            pltpu.VMEM((3, TILES, TILE), f32),
            pltpu.VMEM((2 * NG, NG), bf16),
            message,
            message,
            message,
            message,
            pltpu.VMEM((8, 4, NG), f32),
            message,
            message,
            message,
            *[pltpu.VMEM(t.shape, t.dtype) for t in tables],
            pltpu.SemaphoreType.DMA((len(NAMES),)),
            pltpu.SemaphoreType.DMA,
            pltpu.SemaphoreType.DMA((4,)),
            pltpu.SemaphoreType.DMA((4,)),
            pltpu.SemaphoreType.DMA((4,)),
            pltpu.SemaphoreType.DMA((4,)),
        ],
        compiler_params=pltpu.CompilerParams(
            collective_id=0, has_side_effects=True, vmem_limit_bytes=48 << 20
        ),
        name="forces",
    )(blocks, homes, others, homes.reshape(1, PAIRS), *tables)
    return short.reshape(3, 1, 1, TILES * TILE), long.reshape(3, 1, 1, TILES * TILE)


def solution(mesh):
    tables = make_tables()

    def whole(atoms, pair_home, pair_other):
        fixed = [jnp.asarray(tables[name]) for name in NAMES]
        mapped = jax.shard_map(
            lambda a, h, o: on_device(a, h, o, *fixed),
            mesh=mesh,
            in_specs=(P(None, "grp", "dom", "pen"), P("grp", "dom", "pen"), P("grp", "dom", "pen")),
            out_specs=(P(None, "grp", "dom", "pen"), P(None, "grp", "dom", "pen")),
            check_vma=False,
        )
        return mapped(atoms, pair_home, pair_other)

    return whole
```

time: 257 us -> 76.3 us (0.30)
  starting transfers between devices: 96.6 us -> 0 us
  waiting for transfers between devices: 68.2 us -> 0 us
  Pallas kernels: 0 us -> 65 us
  matrix products: 33.6 us -> 0 us
  other arithmetic: 26.4 us -> 0 us
  blocking collectives: 8.97 us -> 0 us
  local copies, waits for them, and re-layouts: 17.8 us -> 10.2 us
  loops' own time: 3.19 us -> 0 us
    pallas_call x0 -> x1, Pallas kernels: none -> 65 us  [on_device(): pl.pallas_call(kernel, out_shape=(force, force), in_specs=[any_spec, smem...]
    all_to_all x5 -> x0, starting transfers between devices: 54.7 us -> none  [the longest x4 51.4 us: side_by_side(): lax.all_to_all(both, axis, split_axis=split_dim, concat_axis=concat_dim,...]
    all_to_all x5 -> x0, waiting for transfers between devices: 52.3 us -> none  [the longest x4 48 us: side_by_side(): lax.all_to_all(both, axis, split_axis=split_dim, concat_axis=concat_dim,...]
    ppermute x6 -> x0, starting transfers between devices: 41.9 us -> none  [the longest x2 26.8 us: with_halo(): lax.ppermute(lax.slice_in_dim(block, 0, width, axis=dim), axis, backward)]
    dot_general x69 -> x0, matrix products: 33.6 us -> none  [the longest x52 19.5 us: matmul(): jnp.dot(left, right, precision=exact_precision, preferred_element_type=jn...]
    ppermute x6 -> x0, waiting for transfers between devices: 15.9 us -> none  [the longest x2 12.3 us: passed_along(): return lax.ppermute(block, axis, route)]
    reduce_sum x9 -> x0, other arithmetic: 11.9 us -> none  [the longest x4 7.44 us: pair_push(): return jnp.sum(scaled * weight[:, None], axis=3) * home_pos[:, 3:4, :]]
    all_gather x1 -> x0, blocking collectives: 8.97 us -> none  [rows_first(): filled = lax.all_gather(both, axis, axis=0, tiled=True)]
  transfers between devices with their start and end apart: 11 -> 0, of which waited for: 9 -> 0; matrix products, arithmetic and copies ran while one was open for 9% -> 0% of each run, Pallas kernels for 0% -> 0%
where the time goes in v1:
time: 76.3 us; the launch traced here: 75.8 us
  Pallas kernels  65 us (85%)
  local copies, waits for them, and re-layouts  10.2 us (13%)
    pallas_call x1, Pallas kernels, on_device(): pl.pallas_call(kernel, out_shape=(force, force), in_specs=[any_spec, smem...  65 us
    unnamed x24, local copies, waits for them, and re-layouts  10.2 us

profile of v1, /device:TPU:1, one launch (start us, length us, event | category | flops | bytes accessed | tf_op | source)
XLA Modules:
  0.0 75.8 jit_solution(13067937314438476302)
XLA Ops:
  0.6 0.0 copy-start.9
  0.6 0.0 copy-start.10
  0.6 0.6 copy-done.9
  1.3 0.0 copy-done.10
  1.3 0.0 copy-start
  1.3 1.0 %copy-done = bf16[1024,192]{1,0:T(8,128)(2,1)S(1)} copy-done((bf16[1024,192]{1,0:T(8,128)(2,1)S(1)}, bf16[1024,192]{1,0:T(8,128)(2,1)}, u32[]{:S(2)}) %copy-start) | copy-done | bytes 393240
  2.3 0.0 copy-start.1
  2.3 0.9 %copy-done.1 = f32[512,128]{1,0:T(8,128)S(1)} copy-done((f32[512,128]{1,0:T(8,128)S(1)}, f32[512,128]{1,0:T(8,128)}, u32[]{:S(2)}) %copy-start.1) | copy-done | bytes 262168
  3.3 0.0 copy-start.2
  3.3 0.9 %copy-done.2 = bf16[1024,128]{1,0:T(8,128)(2,1)S(1)} copy-done((bf16[1024,128]{1,0:T(8,128)(2,1)S(1)}, bf16[1024,128]{1,0:T(8,128)(2,1)}, u32[]{:S(2)}) %copy-start.2) | copy-done | bytes 262168
  4.2 0.0 copy-start.3
  4.2 0.9 %copy-done.3 = bf16[128,1024]{1,0:T(8,128)(2,1)S(1)} copy-done((bf16[128,1024]{1,0:T(8,128)(2,1)S(1)}, bf16[128,1024]{1,0:T(8,128)(2,1)}, u32[]{:S(2)}) %copy-start.3) | copy-done | bytes 262168
  5.2 0.0 copy-start.4
  5.2 0.9 %copy-done.4 = bf16[1024,96]{1,0:T(8,128)(2,1)S(1)} copy-done((bf16[1024,96]{1,0:T(8,128)(2,1)S(1)}, bf16[1024,96]{1,0:T(8,128)(2,1)}, u32[]{:S(2)}) %copy-start.4) | copy-done | bytes 196632
  6.1 0.0 copy-start.5
  6.1 0.9 %copy-done.5 = bf16[512,128]{1,0:T(8,128)(2,1)S(1)} copy-done((bf16[512,128]{1,0:T(8,128)(2,1)S(1)}, bf16[512,128]{1,0:T(8,128)(2,1)}, u32[]{:S(2)}) %copy-start.5) | copy-done | bytes 131096
  7.1 0.0 copy-start.6
  7.1 0.9 %copy-done.6 = bf16[64,1024]{1,0:T(8,128)(2,1)S(1)} copy-done((bf16[64,1024]{1,0:T(8,128)(2,1)S(1)}, bf16[64,1024]{1,0:T(8,128)(2,1)}, u32[]{:S(2)}) %copy-start.6) | copy-done | bytes 131096
  8.0 0.0 copy-start.7
  8.0 0.8 %copy-done.7 = f32[4,1,1,4096]{3,2,1,0:T(1,128)S(1)} copy-done((f32[4,1,1,4096]{3,2,1,0:T(1,128)S(1)}, f32[4,1,1,4096]{3,2,1,0:T(1,128)}, u32[]{:S(2)}) %copy-start.7) | copy-done | bytes 65560
  8.8 0.0 copy-start.8
  8.8 0.8 %copy-done.8 = bf16[256,128]{1,0:T(8,128)(2,1)S(1)} copy-done((bf16[256,128]{1,0:T(8,128)(2,1)S(1)}, bf16[256,128]{1,0:T(8,128)(2,1)}, u32[]{:S(2)}) %copy-start.8) | copy-done | bytes 65560
  9.6 65.0 %forces.1 = (f32[3,32,128]{2,1,0:T(8,128)S(1)}, f32[3,32,128]{2,1,0:T(8,128)S(1)}) custom-call(f32[4,32,128]{2,1,0:T(8,128)S(1)} %bitcast.6, s32[64]{0:T(128)S(1)} %bitcast.9, s32[64]{0:T(128)S(1)} %bitcast.11, s32[1,64]{1,0:T(1,128)S(1)} %bitcast.10, bf16[256,128]{1,0:T(8,128)(2,1)S(1)} %copy-done.8, bf16[1024,192]{1,0:T(8,128)(2,1)S(1)} %copy-done, ...), custom_call_target="tpu_custom_call" | custom-call | tf_op jit(solution)/shard_map/forces/pallas_call | solution.py:561
  74.6 0.6 copy.19
  75.2 0.6 copy.20
Async XLA Ops:
  0.6 0.7 copy-start.9
  0.6 0.7 copy-start.10
  1.3 1.0 %copy-start = (bf16[1024,192]{1,0:T(8,128)(2,1)S(1)}, bf16[1024,192]{1,0:T(8,128)(2,1)}, u32[]{:S(2)}) copy-start(bf16[1024,192]{1,0:T(8,128)(2,1)} %constant.17.clone.fx_hbm) | copy-start | bytes 1179652
  2.3 0.9 %copy-start.1 = (f32[512,128]{1,0:T(8,128)S(1)}, f32[512,128]{1,0:T(8,128)}, u32[]{:S(2)}) copy-start(f32[512,128]{1,0:T(8,128)} %constant.23.clone.parts_hbm) | copy-start | bytes 786436
  3.3 0.9 %copy-start.2 = (bf16[1024,128]{1,0:T(8,128)(2,1)S(1)}, bf16[1024,128]{1,0:T(8,128)(2,1)}, u32[]{:S(2)}) copy-start(bf16[1024,128]{1,0:T(8,128)(2,1)} %constant.21.clone.px_hbm) | copy-start | bytes 786436
  4.2 0.9 %copy-start.3 = (bf16[128,1024]{1,0:T(8,128)(2,1)S(1)}, bf16[128,1024]{1,0:T(8,128)(2,1)}, u32[]{:S(2)}) copy-start(bf16[128,1024]{1,0:T(8,128)(2,1)} %constant.19.clone.ix_hbm) | copy-start | bytes 786436
  5.2 0.9 %copy-start.4 = (bf16[1024,96]{1,0:T(8,128)(2,1)S(1)}, bf16[1024,96]{1,0:T(8,128)(2,1)}, u32[]{:S(2)}) copy-start(bf16[1024,96]{1,0:T(8,128)(2,1)} %constant.18.clone.fy_hbm) | copy-start | bytes 589828
  6.1 0.9 %copy-start.5 = (bf16[512,128]{1,0:T(8,128)(2,1)S(1)}, bf16[512,128]{1,0:T(8,128)(2,1)}, u32[]{:S(2)}) copy-start(bf16[512,128]{1,0:T(8,128)(2,1)} %constant.22.clone.py_hbm) | copy-start | bytes 393220
  7.1 0.9 %copy-start.6 = (bf16[64,1024]{1,0:T(8,128)(2,1)S(1)}, bf16[64,1024]{1,0:T(8,128)(2,1)}, u32[]{:S(2)}) copy-start(bf16[64,1024]{1,0:T(8,128)(2,1)} %constant.20.clone.iy_hbm) | copy-start | bytes 393220
  8.0 0.8 %copy-start.7 = (f32[4,1,1,4096]{3,2,1,0:T(1,128)S(1)}, f32[4,1,1,4096]{3,2,1,0:T(1,128)}, u32[]{:S(2)}) copy-start(f32[4,1,1,4096]{3,2,1,0:T(1,128)} %param.11) | copy-start | bytes 196612
  8.8 0.8 %copy-start.8 = (bf16[256,128]{1,0:T(8,128)(2,1)S(1)}, bf16[256,128]{1,0:T(8,128)(2,1)}, u32[]{:S(2)}) copy-start(bf16[256,128]{1,0:T(8,128)(2,1)} %constant.16.clone.basis_hbm) | copy-start | bytes 196612

commit v2 on v1

--- a/solution.py
+++ b/solution.py
@@ -54,9 +54,17 @@
     return out.reshape(inner * 2 * NG, count * inner)
 
 
+def patch_places():
+    places = [(x, y) for y in range(SIDE) for x in range(8)]
+    places += [(x, y) for x in range(8, SIDE) for y in range(8)]
+    places += [(x, y) for x in range(8, SIDE) for y in range(8, SIDE)]
+    places += [(SIDE, SIDE)] * (NG - len(places))
+    return np.array(places).T
+
+
 def make_tables():
     row = np.arange(NG)
-    row_x, row_y = row // SIDE, row % SIDE
+    row_x, row_y = patch_places()
     lane_z, lane_y = (row // 16) % 2, row % 16
     x_c, x_s, bx_c, bx_s = turning(8 * np.arange(16), row_x - 3, row < SIDE * SIDE)
     y_c, y_s, by_c, by_s = turning(8 * np.arange(8), 64 * lane_z - 3 + lane_y, lane_y < SIDE)
@@ -78,25 +86,27 @@
             pick_y[i, lane, i * 4 + lane // 32] = 1.0
     zh, zl = halves(basis(row))
     return dict(
-        basis_z=np.concatenate([zh, zl], axis=0),
         forward_x=forward_x,
         forward_y=forward_y,
-        inverse_x=inverse_x,
-        inverse_y=inverse_y,
-        pick_x=pick_x.reshape(1024, NG).astype(jnp.bfloat16),
-        pick_y=pick_y.reshape(512, NG).astype(jnp.bfloat16),
+        inverse=np.concatenate([inverse_x, inverse_y], axis=0),
+        picks=np.concatenate(
+            [
+                pick_x.reshape(1024, NG).astype(jnp.bfloat16),
+                pick_y.reshape(512, NG).astype(jnp.bfloat16),
+                zh,
+                zl,
+            ],
+            axis=0,
+        ),
         parts=np.concatenate([bx_c, bx_s, by_c, by_s], axis=0).astype(np.float32),
     )
 
 
 NAMES = (
-    "basis_z",
+    "picks",
     "forward_x",
     "forward_y",
-    "inverse_x",
-    "inverse_y",
-    "pick_x",
-    "pick_y",
+    "inverse",
     "parts",
 )
 
@@ -234,43 +244,53 @@
     return jnp.where(square > 0.5, value, 0.0)
 
 
-def pair_push(home, other, scales):
-    scaled = []
-    for c in range(3):
-        delta = home[c] - other[:, c : c + 1]
-        delta = delta - jnp.floor(delta + 0.5)
-        scaled.append(delta * scales[c])
-    square = scaled[0] * scaled[0] + scaled[1] * scaled[1] + scaled[2] * scaled[2]
-    weight = jnp.exp(-0.5 * square) * other[:, 3:4]
-    return [jnp.sum(s * weight, axis=0, keepdims=True) for s in scaled]
-
-
-LOW = 0
-THETA = 3
-SLOPE = 15
-CHARGED = 27
-FIELDS = 31
+def thirds(x):
+    high = x.astype(bf16).astype(f32)
+    rest = x - high
+    middle = rest.astype(bf16).astype(f32)
+    return high, middle, rest - middle
+
+
+def pair_push(other, against):
+    columns = jnp.concatenate([*thirds(other), jnp.ones_like(other)], axis=0).astype(bf16)
+    wide = lax.dot_general(
+        columns, against, (((0,), (0,)), ((), ())), preferred_element_type=f32
+    )
+    delta = [wide[:, 128 * c : 128 * c + 128] for c in range(3)]
+    delta[2] = delta[2] - jnp.floor(delta[2] + 0.5)
+    square = delta[0] * delta[0] + delta[1] * delta[1] + delta[2] * delta[2]
+    weight = jnp.exp2(square * (-512.0 * math.log2(math.e))) * wide[:, 384:]
+    return [jnp.sum(d * weight, axis=0, keepdims=True) for d in delta]
+
+
+PLACE = 0
+THETA = 12
+SLOPE = 24
+CHARGED = 36
+Z_LOW = 40
+FIELDS = 48
 
 
 def kernel(
     atoms_hbm,
+    home_hbm,
+    other_hbm,
+    home_row_hbm,
+    picks_hbm,
+    fx_hbm,
+    fy_hbm,
+    inverse_hbm,
+    parts_hbm,
+    short_ref,
+    long_ref,
     home_smem,
     other_smem,
     home_vmem,
-    basis_hbm,
-    fx_hbm,
-    fy_hbm,
-    ix_hbm,
-    iy_hbm,
-    px_hbm,
-    py_hbm,
-    parts_hbm,
-    short_ref,
-    long_ref,
     near,
     fields,
     mesh,
     pushes,
+    against,
     grads,
     pot_parts,
     send_a,
@@ -281,13 +301,10 @@
     recv_c,
     send_d,
     recv_d,
-    basis_z,
+    picks,
     forward_x,
     forward_y,
-    inverse_x,
-    inverse_y,
-    pick_x,
-    pick_y,
+    inverse,
     parts,
     table_sems,
     atom_sem,
@@ -299,17 +316,17 @@
     grp = lax.axis_index("grp")
     dom = lax.axis_index("dom")
     pen = lax.axis_index("pen")
-    z_hi, y_at = pen // 8, lax.rem(pen, 8)
+    z_hi, y_at = pen >> 3, pen & 7
     at_a = z_hi * 16 + dom
     at_b = grp * 8 + y_at
 
     def peer_a(k):
-        t = lax.rem(at_a + k, PEERS)
-        return t, {"grp": grp, "dom": lax.rem(t, 16), "pen": (t // 16) * 8 + y_at}
+        t = (at_a + k) & (PEERS - 1)
+        return t, {"grp": grp, "dom": t & 15, "pen": (t >> 4) * 8 + y_at}
 
     def peer_b(k):
-        b = lax.rem(at_b + k, PEERS)
-        return b, {"grp": b // 8, "dom": dom, "pen": z_hi * 8 + lax.rem(b, 8)}
+        b = (at_b + k) & (PEERS - 1)
+        return b, {"grp": b >> 3, "dom": dom, "pen": z_hi * 8 + (b & 7)}
 
     pen_next = {"grp": grp, "dom": dom, "pen": lax.rem(pen + 1, 16)}
     pen_prev = {"grp": grp, "dom": dom, "pen": lax.rem(pen + 15, 16)}
@@ -325,7 +342,7 @@
         pl.semaphore_signal(barrier, 1, device_id=peer_b(k)[1], device_id_type=MESH)
         return carry
 
-    lax.fori_loop(1, PEERS, greet, 0)
+    lax.fori_loop(1, PEERS, greet, 0, unroll=True)
     pl.semaphore_signal(barrier, 1, device_id=pen_next, device_id_type=MESH)
     pl.semaphore_signal(barrier, 1, device_id=pen_prev, device_id_type=MESH)
 
@@ -333,14 +350,14 @@
         pltpu.make_async_copy(source, target, table_sems.at[n])
         for n, (source, target) in enumerate(
             (
-                (basis_hbm, basis_z),
+                (picks_hbm, picks),
                 (fx_hbm, forward_x),
                 (fy_hbm, forward_y),
-                (ix_hbm, inverse_x),
-                (iy_hbm, inverse_y),
-                (px_hbm, pick_x),
-                (py_hbm, pick_y),
+                (inverse_hbm, inverse),
                 (parts_hbm, parts),
+                (home_hbm, home_smem),
+                (other_hbm, other_smem),
+                (home_row_hbm, home_vmem),
             )
         )
     ]
@@ -351,40 +368,66 @@
     charge = near[4, 3]
     for c, start in ((0, (dom * 8).astype(f32)), (1, (pen * 8).astype(f32)), (2, 3.0)):
         floored, thetas, slopes = spline_terms(near[4, c] * float(NG))
-        fields[LOW + c] = floored - start
+        lowest = floored - start
         for k in range(4):
-            fields[THETA + 4 * c + k] = thetas[k]
-            fields[SLOPE + 4 * c + k] = slopes[k]
+            place = lowest + float(k)
+            theta, slope = thetas[k], slopes[k]
             if c == 1:
-                fields[CHARGED + k] = thetas[k] * charge
-
-    column = lax.broadcasted_iota(jnp.int32, (NG, TILE), 0)
-    patch_x = jnp.floor((column.astype(f32) + 0.5) * (1.0 / SIDE))
-    patch_y = column.astype(f32) - SIDE * patch_x
+                fields[CHARGED + k] = theta * charge
+            if c == 2:
+                place = jnp.where(place < 0.0, place + float(NG), place)
+                high = theta.astype(bf16).astype(f32)
+                fields[Z_LOW + k] = theta - high
+                theta = high
+                high = slope.astype(bf16).astype(f32)
+                fields[Z_LOW + 4 + k] = slope - high
+                slope = high
+            fields[PLACE + 4 * c + k] = place
+            fields[THETA + 4 * c + k] = theta
+            fields[SLOPE + 4 * c + k] = slope
+
+    z_at = lax.broadcasted_iota(jnp.int32, (NG, TILE), 0).astype(f32).astype(bf16)
+    side_at = lax.broadcasted_iota(jnp.int32, (16, TILE), 0).astype(f32)
+    corner_at = jnp.minimum(lax.broadcasted_iota(jnp.int32, (16, TILE), 0), 9).astype(f32)
+    corner_x = jnp.floor((corner_at + 0.5) * (1.0 / 3.0))
+    corner_y = 8.0 + corner_at - 3.0 * corner_x
+    corner_x = corner_x + 8.0
 
     def row(field, tile):
         return fields[field, pl.ds(tile, 1), :]
 
+    def rows_of(field, tile):
+        return [row(field + k, tile) for k in range(4)]
+
+    def narrow(field, tile):
+        return [r.astype(bf16) for r in rows_of(field, tile)]
+
     def at_z(tile):
-        return matches((column - row(LOW + 2, tile).astype(jnp.int32)) & (NG - 1))
+        return [z_at == r for r in narrow(PLACE + 8, tile)]
+
+    def at(axis, where, tile):
+        return [where == r for r in rows_of(PLACE + 4 * axis, tile)]
+
+    def across(value, n):
+        return jnp.broadcast_to(value[n : n + 1], (8, TILE))
 
     mesh[...] = jnp.zeros_like(mesh)
 
     def spread(step, carry):
-        z_parts, p_parts = [], []
+        z_high, z_low, p_parts = [], [], []
         for n in range(4):
             tile = step * 4 + n
-            w_z = one_of(at_z(tile), [row(THETA + 8 + k, tile) for k in range(4)])
-            w_x = one_of(
-                matches(patch_x - row(LOW, tile)), [row(THETA + k, tile) for k in range(4)]
-            )
-            w_y = one_of(
-                matches(patch_y - row(LOW + 1, tile)), [row(CHARGED + k, tile) for k in range(4)]
-            )
-            z_parts.append(split(w_z))
-            p_parts.append(split(w_x * w_y))
-        z_high = jnp.concatenate([z[0] for z in z_parts], axis=1)
-        z_low = jnp.concatenate([z[1] for z in z_parts], axis=1)
+            is_z = at_z(tile)
+            z_high.append(one_of(is_z, narrow(THETA + 8, tile)))
+            z_low.append(one_of(is_z, narrow(Z_LOW, tile)))
+            t_x, t_y = rows_of(THETA, tile), rows_of(CHARGED, tile)
+            w_x, w_y = one_of(at(0, side_at, tile), t_x), one_of(at(1, side_at, tile), t_y)
+            pieces = [w_x[:8] * across(w_y, y) for y in range(SIDE)]
+            pieces += [across(w_x, x) * w_y[:8] for x in range(8, SIDE)]
+            pieces += [one_of(at(0, corner_x, tile), t_x) * one_of(at(1, corner_y, tile), t_y)]
+            p_parts.append(split(jnp.concatenate(pieces, axis=0)))
+        z_high = jnp.concatenate(z_high, axis=1)
+        z_low = jnp.concatenate(z_low, axis=1)
         p_high = jnp.concatenate([p[0] for p in p_parts], axis=1)
         p_low = jnp.concatenate([p[1] for p in p_parts], axis=1)
         wide = dot_nt(z_high, jnp.concatenate([p_high, p_low], axis=0))
@@ -427,13 +470,13 @@
             device_id_type=MESH,
         )
         both.wait_recv()
-        both.wait_send()
+        return both
 
     def same(index):
         return index
 
     loads[0].wait()
-    put(send_a, to_z(mesh[...], basis_z[...]))
+    put(send_a, to_z(mesh[...], picks[1536:]))
     pl.semaphore_wait(barrier, 2 * (PEERS - 1) + 2)
     exchange(send_a, recv_a, 0, peer_a, at_a, same)
 
@@ -448,8 +491,39 @@
         )
 
     side = [halo(4, 3, 0, pen_next), halo(4, 5, 1, pen_prev)]
-    for copy in side:
-        copy.start()
+    pl.when(y_at != 7)(side[0].start)
+    pl.when(y_at != 0)(side[1].start)
+    ends = [
+        halo(slot, slot - 3 if up else slot + 3, 2 + 2 * n + up, device)
+        for n, slot in enumerate((3, 4, 5))
+        for up, device in enumerate((dom_prev, dom_next))
+    ]
+
+    def hand_on(n):
+        if n != 1:
+            side[n // 2].wait_recv()
+        for copy in ends[2 * n : 2 * n + 2]:
+            copy.start()
+
+    table_row = lax.broadcasted_iota(jnp.int32, (16, 4 * TILE), 0)
+    table_block = lax.broadcasted_iota(jnp.int32, (16, 4 * TILE), 1) >> 7
+    table_sign = jnp.where(table_block == 3, 1.0, -1.0)
+    table_fixed = jnp.where(((table_row & 3) == table_block) & (table_row < 12), table_sign, 0.0)
+
+    def home_table(tile, carry):
+        rows = [near[4, c, pl.ds(tile, 1), :] for c in range(3)]
+        filled = table_fixed
+        parts_of = thirds(jnp.concatenate(rows + [jnp.zeros_like(rows[0])], axis=1))
+        for k in range(3):
+            filled = jnp.where(table_row == 12 + k, parts_of[k], filled)
+        against[tile] = filled.astype(bf16)
+        return carry
+
+    lax.fori_loop(0, TILES, home_table, 0, unroll=2)
+
+    pl.delay(2400)
+    pl.when(y_at == 7)(side[0].start)
+    pl.when(y_at == 0)(side[1].start)
 
     for load in loads[1:]:
         load.wait()
@@ -463,61 +537,66 @@
 
     peer_one_a = peer_a(1)[1]
     peer_one_b = peer_b(1)[1]
-    arrived(recv_a, 0, peer_one_a)
-    put(send_b, to_lines_x(taken(recv_a), forward_x[...], part_xc, part_xs, pick_x[...]))
+    sent_0 = arrived(recv_a, 0, peer_one_a)
+    put(send_b, to_lines_x(taken(recv_a), forward_x[...], part_xc, part_xs, picks[:1024]))
     exchange(send_b, recv_b, 1, peer_b, at_b, same)
-
-    arrived(recv_b, 1, peer_one_b)
+    hand_on(1)
+    pl.when(y_at != 0)(lambda: hand_on(0))
+    pl.when(y_at != 7)(lambda: hand_on(2))
+
+    sent_1 = arrived(recv_b, 1, peer_one_b)
     put(
         send_c,
         through_y(
             taken(recv_b),
             factor,
             forward_y[...],
-            inverse_y[...],
+            inverse[128:],
             part_yc,
             part_ys,
-            pick_y[...],
+            picks[1024:1536],
         ),
     )
-    exchange(send_c, recv_c, 2, peer_b, at_b, lambda index: lax.rem(index, 8))
-
-    for copy in side:
-        copy.wait()
-    ends = [
-        halo(pl.ds(3, 3), pl.ds(0, 3), 2, dom_next),
-        halo(pl.ds(3, 3), pl.ds(6, 3), 3, dom_prev),
-    ]
-    for copy in ends:
-        copy.start()
-
-    arrived(recv_c, 2, peer_one_b)
-    put(send_d, from_lines_x(taken(recv_c), inverse_x[...], part_xc, part_xs, pick_x[...]))
+    exchange(send_c, recv_c, 2, peer_b, at_b, lambda index: index & 7)
+
+    pl.when(y_at == 0)(lambda: hand_on(0))
+    pl.when(y_at == 7)(lambda: hand_on(2))
+
+    sent_2 = arrived(recv_c, 2, peer_one_b)
+    put(send_d, from_lines_x(taken(recv_c), inverse[:128], part_xc, part_xs, picks[:1024]))
     exchange(send_d, recv_d, 3, peer_a, at_a, same)
 
     for copy in ends:
         copy.wait()
-    scales = (32.0, 32.0, 32.0)
-    pad = jnp.zeros((4, TILE), f32)
+    for copy in side:
+        copy.wait_send()
+    def period(step, at_edge):
+        below = (step == -1) & (at_edge == 0)
+        above = (step == 1) & (at_edge == 15)
+        return jnp.where(below, 1.0, jnp.where(above, -1.0, 0.0)).astype(f32)
 
     def pair(n, carry):
         home, other = home_smem[n], other_smem[n]
-        own = [near[4, c, pl.ds(home, 1), :] for c in range(3)]
-        far = [near[other >> 5, c, pl.ds(other & 31, 1), :] for c in range(4)]
-        rows = pair_push(own, jnp.concatenate(far + [pad], axis=0).T, scales)
+        block, tile = other >> 5, other & 31
+        step_d = jnp.where(block < 3, -1, jnp.where(block < 6, 0, 1))
+        step_p = block - 3 * (step_d + 1) - 1
+        far = [near[block, c, pl.ds(tile, 1), :] for c in range(4)]
+        far[0] = far[0] - period(step_d, dom)
+        far[1] = far[1] - period(step_p, pen)
+        rows = pair_push(jnp.concatenate(far, axis=0), against[home])
         for c in range(3):
             pushes[c, pl.ds(n, 1), :] = rows[c]
         return carry
 
-    lax.fori_loop(0, PAIRS, pair, 0, unroll=2)
+    lax.fori_loop(0, PAIRS, pair, 0, unroll=4)
     tile_ids = lax.broadcasted_iota(jnp.int32, (TILES, PAIRS), 0)
     owners = jnp.where(home_vmem[...] == tile_ids, 1.0, 0.0).astype(bf16)
     for c in range(3):
         high, low = split(pushes[c])
-        short_ref[c] = (dot(owners, high) + dot(owners, low)) * (charge * (2.0 / math.sqrt(256.0)))
-
-    arrived(recv_d, 3, peer_one_a)
-    pot_high, pot_low = split(from_z(taken(recv_d), basis_z[...]))
+        short_ref[c] = (dot(owners, high) + dot(owners, low)) * (charge * (32.0 * 2.0 / math.sqrt(256.0)))
+
+    sent_3 = arrived(recv_d, 3, peer_one_a)
+    pot_high, pot_low = split(from_z(taken(recv_d), picks[1536:]))
     pot_parts[:128] = pot_high
     pot_parts[128:] = pot_low
 
@@ -525,24 +604,43 @@
         for n in range(2):
             tile = step * 2 + n
             is_z = at_z(tile)
-            w_z = one_of(is_z, [row(THETA + 8 + k, tile) for k in range(4)])
-            s_z = one_of(is_z, [row(SLOPE + 8 + k, tile) for k in range(4)])
-            high, low = split(jnp.concatenate([w_z, s_z], axis=1))
-            full = dot(pot_parts[...], high)
-            along = full[:128] + full[128:] + dot(pot_parts[:128], low)
-            is_x = matches(patch_x - row(LOW, tile))
-            w_x = one_of(is_x, [row(THETA + k, tile) for k in range(4)])
-            s_x = one_of(is_x, [row(SLOPE + k, tile) for k in range(4)])
-            is_y = matches(patch_y - row(LOW + 1, tile))
-            w_y = one_of(is_y, [row(THETA + 4 + k, tile) for k in range(4)])
-            s_y = one_of(is_y, [row(SLOPE + 4 + k, tile) for k in range(4)])
-            value, slope = along[:, :128], along[:, 128:]
-            sums = (s_x * (w_y * value), w_x * (s_y * value), w_x * (w_y * slope))
+            high = [one_of(is_z, narrow(THETA + 8, tile)), one_of(is_z, narrow(SLOPE + 8, tile))]
+            low = [one_of(is_z, narrow(Z_LOW, tile)), one_of(is_z, narrow(Z_LOW + 4, tile))]
+            full = dot(pot_parts[...], jnp.concatenate(high, axis=1))
+            along = full[:128] + full[128:] + dot(pot_parts[:128], jnp.concatenate(low, axis=1))
+            value = [along[8 * k : 8 * k + 8, :128] for k in range(16)]
+            slope = [along[8 * k : 8 * k + 8, 128:] for k in range(16)]
+            t_x, d_x = rows_of(THETA, tile), rows_of(SLOPE, tile)
+            t_y, d_y = rows_of(THETA + 4, tile), rows_of(SLOPE + 4, tile)
+            is_x, is_y = at(0, side_at, tile), at(1, side_at, tile)
+            w_x, s_x = one_of(is_x, t_x), one_of(is_x, d_x)
+            w_y, s_y = one_of(is_y, t_y), one_of(is_y, d_y)
+            by_y = [[], [], []]
+            for y in range(SIDE):
+                by_y[0].append(across(w_y, y) * value[y])
+                by_y[1].append(across(s_y, y) * value[y])
+                by_y[2].append(across(w_y, y) * slope[y])
+            by_x = [[], [], []]
+            for x in range(8, SIDE):
+                by_x[0].append(across(s_x, x) * value[x + 3])
+                by_x[1].append(across(w_x, x) * value[x + 3])
+                by_x[2].append(across(w_x, x) * slope[x + 3])
+            is_x, is_y = at(0, corner_x, tile), at(1, corner_y, tile)
+            cw_x, cs_x = one_of(is_x, t_x), one_of(is_x, d_x)
+            cw_y, cs_y = one_of(is_y, t_y), one_of(is_y, d_y)
+            ends_x, ends_y = (s_x, w_x, w_x), (w_y, s_y, w_y)
             for c in range(3):
-                grads[c, pl.ds(tile, 1), :] = jnp.sum(sums[c], axis=0, keepdims=True)
+                total = ends_x[c][:8] * sum(by_y[c][1:], by_y[c][0])
+                total += ends_y[c][:8] * sum(by_x[c][1:], by_x[c][0])
+                own = slope if c == 2 else value
+                corner = (cs_x * cw_y, cw_x * cs_y, cw_x * cw_y)[c]
+                total += corner[:8] * own[14] + corner[8:] * own[15]
+                grads[c, pl.ds(tile, 1), :] = jnp.sum(total, axis=0, keepdims=True)
         return carry
 
     lax.fori_loop(0, TILES // 2, interpolate, 0)
+    for sent in (sent_0, sent_1, sent_2, sent_3):
+        sent.wait_send()
     total_atoms = 4 * 16 * 16 * 4096
     scale = -0.4 * NG / math.sqrt(NG * total_atoms)
     for c in range(3):
@@ -550,8 +648,7 @@
 
 
 def on_device(atoms, pair_home, pair_other, *tables):
-    any_spec = pl.BlockSpec(memory_space=pl.ANY)
-    smem = pl.BlockSpec(memory_space=pltpu.SMEM)
+    hbm = pl.BlockSpec(memory_space=pl.ANY)
     vmem = pl.BlockSpec(memory_space=pltpu.VMEM)
     blocks = atoms.reshape(4, TILES, TILE)
     homes = pair_home.reshape(PAIRS)
@@ -561,13 +658,17 @@
     short, long = pl.pallas_call(
         kernel,
         out_shape=(force, force),
-        in_specs=[any_spec, smem, smem, vmem] + [any_spec] * len(NAMES),
+        in_specs=[hbm] * (4 + len(NAMES)),
         out_specs=(vmem, vmem),
         scratch_shapes=[
+            pltpu.SMEM((PAIRS,), jnp.int32),
+            pltpu.SMEM((PAIRS,), jnp.int32),
+            pltpu.VMEM((1, PAIRS), jnp.int32),
             pltpu.VMEM((9, 4, TILES, TILE), f32),
             pltpu.VMEM((FIELDS, TILES, TILE), f32),
             pltpu.VMEM((NG, NG), f32),
             pltpu.VMEM((3, PAIRS, TILE), f32),
+            pltpu.VMEM((TILES, 16, 4 * TILE), bf16),
             pltpu.VMEM((3, TILES, TILE), f32),
             pltpu.VMEM((2 * NG, NG), bf16),
             message,
@@ -579,15 +680,15 @@
             message,
             message,
             *[pltpu.VMEM(t.shape, t.dtype) for t in tables],
-            pltpu.SemaphoreType.DMA((len(NAMES),)),
+            pltpu.SemaphoreType.DMA((len(NAMES) + 3,)),
             pltpu.SemaphoreType.DMA,
             pltpu.SemaphoreType.DMA((4,)),
             pltpu.SemaphoreType.DMA((4,)),
-            pltpu.SemaphoreType.DMA((4,)),
-            pltpu.SemaphoreType.DMA((4,)),
+            pltpu.SemaphoreType.DMA((8,)),
+            pltpu.SemaphoreType.DMA((8,)),
         ],
         compiler_params=pltpu.CompilerParams(
-            collective_id=0, has_side_effects=True, vmem_limit_bytes=48 << 20
+            collective_id=0, has_side_effects=True, vmem_limit_bytes=56_400_000
         ),
         name="forces",
     )(blocks, homes, others, homes.reshape(1, PAIRS), *tables)

time: 76.3 us -> 61.4 us (0.80)
  local copies, waits for them, and re-layouts: 10.2 us -> 1.9 us
  Pallas kernels: 65 us -> 58.6 us
    unnamed x24 -> x6, local copies, waits for them, and re-layouts: 10.2 us -> 1.9 us
    pallas_call x1, Pallas kernels: 65 us -> 58.6 us  [on_device(): pl.pallas_call(kernel, out_shape=(force, force), in_specs=[hbm] * (4 + le...]
where the time goes in v2:
time: 61.4 us; the launch traced here: 61.2 us
  Pallas kernels  58.6 us (95%)
  local copies, waits for them, and re-layouts  1.9 us (3%)
  between operations  0.66 us (1%)
    pallas_call x1, Pallas kernels, on_device(): pl.pallas_call(kernel, out_shape=(force, force), in_specs=[hbm] * (4 + le...  58.6 us
    unnamed x6, local copies, waits for them, and re-layouts  1.9 us

profile of v2, /device:TPU:1, one launch (start us, length us, event | category | flops | bytes accessed | tf_op | source)
XLA Modules:
  0.0 61.2 jit_solution(1340663269017317670)
XLA Ops:
  0.6 0.0 copy-start
  0.6 0.0 copy-start.1
  0.6 0.6 %copy-done = s32[1,1,64]{2,1,0:T(1,128)S(1)} copy-done((s32[1,1,64]{2,1,0:T(1,128)S(1)}, s32[1,1,64]{2,1,0:T(1,128)}, u32[]{:S(2)}) %copy-start) | copy-done | bytes 280
  1.3 0.0 copy-done.1
  1.3 58.6 %forces.1 = (f32[3,32,128]{2,1,0:T(8,128)S(1)}, f32[3,32,128]{2,1,0:T(8,128)S(1)}) custom-call(f32[4,32,128]{2,1,0:T(8,128)} %bitcast.11, s32[64]{0:T(128)S(1)} %bitcast.8, s32[64]{0:T(128)S(1)} %bitcast.10, s32[1,64]{1,0:T(1,128)S(1)} %bitcast.9, bf16[1792,128]{1,0:T(8,128)(2,1)} %constant.10.clone.picks_hbm, bf16[1024,192]{1,0:T(8,128)(2,1)} %constant.11.clone.fx_hbm, ...), custom_call_target="tpu_custom_call" | custom-call | tf_op jit(solution)/shard_map/forces/pallas_call | solution.py:658
  59.9 0.6 %copy.16 = f32[3,1,1,4096]{3,2,1,0:T(1,128)} copy(f32[3,1,1,4096]{3,2,1,0:T(1,128)S(1)} %bitcast.7) | data formatting | bytes 98304
  60.5 0.6 %copy.17 = f32[3,1,1,4096]{3,2,1,0:T(1,128)} copy(f32[3,1,1,4096]{3,2,1,0:T(1,128)S(1)} %bitcast.6) | data formatting | bytes 98304
Async XLA Ops:
  0.6 0.7 %copy-start = (s32[1,1,64]{2,1,0:T(1,128)S(1)}, s32[1,1,64]{2,1,0:T(1,128)}, u32[]{:S(2)}) copy-start(s32[1,1,64]{2,1,0:T(1,128)} %param.9) | copy-start | bytes 772
  0.6 0.7 %copy-start.1 = (s32[1,1,64]{2,1,0:T(1,128)S(1)}, s32[1,1,64]{2,1,0:T(1,128)}, u32[]{:S(2)}) copy-start(s32[1,1,64]{2,1,0:T(1,128)} %param.10) | copy-start | bytes 772

commit v3 on v2

--- a/solution.py
+++ b/solution.py
@@ -293,6 +293,8 @@
     against,
     grads,
     pot_parts,
+    z_table,
+    xy_table,
     send_a,
     recv_a,
     send_b,
@@ -325,8 +327,8 @@
         return t, {"grp": grp, "dom": t & 15, "pen": (t >> 4) * 8 + y_at}
 
     def peer_b(k):
-        b = (at_b + k) & (PEERS - 1)
-        return b, {"grp": b >> 3, "dom": dom, "pen": z_hi * 8 + (b & 7)}
+        to_grp, to_y = (grp + (k >> 3)) & 3, (y_at + (k & 7)) & 7
+        return to_grp * 8 + to_y, {"grp": to_grp, "dom": dom, "pen": z_hi * 8 + to_y}
 
     pen_next = {"grp": grp, "dom": dom, "pen": lax.rem(pen + 1, 16)}
     pen_prev = {"grp": grp, "dom": dom, "pen": lax.rem(pen + 15, 16)}
@@ -337,12 +339,11 @@
     load_atoms.start()
     barrier = pltpu.get_barrier_semaphore()
 
-    def greet(k, carry):
+    for n in range(1, PEERS):
+        k = 16 + (n >> 1) * (1 if n & 1 else -1)
         pl.semaphore_signal(barrier, 1, device_id=peer_a(k)[1], device_id_type=MESH)
+    for k in range(1, PEERS):
         pl.semaphore_signal(barrier, 1, device_id=peer_b(k)[1], device_id_type=MESH)
-        return carry
-
-    lax.fori_loop(1, PEERS, greet, 0, unroll=True)
     pl.semaphore_signal(barrier, 1, device_id=pen_next, device_id_type=MESH)
     pl.semaphore_signal(barrier, 1, device_id=pen_prev, device_id_type=MESH)
 
@@ -420,6 +421,8 @@
             is_z = at_z(tile)
             z_high.append(one_of(is_z, narrow(THETA + 8, tile)))
             z_low.append(one_of(is_z, narrow(Z_LOW, tile)))
+            z_table[tile, :128, :128] = z_high[-1]
+            z_table[tile, 128:, :128] = z_low[-1]
             t_x, t_y = rows_of(THETA, tile), rows_of(CHARGED, tile)
             w_x, w_y = one_of(at(0, side_at, tile), t_x), one_of(at(1, side_at, tile), t_y)
             pieces = [w_x[:8] * across(w_y, y) for y in range(SIDE)]
@@ -443,9 +446,9 @@
     def taken(ref):
         return jnp.concatenate([ref[n] for n in range(PEERS)], axis=0)
 
-    def exchange(source, target, phase, peer, own, slot):
+    def exchange(source, target, phase, peer, own, slot, offset):
         def post(k, carry):
-            index, device = peer(k)
+            index, device = peer(offset(k))
             pltpu.make_async_remote_copy(
                 src_ref=source.at[slot(index)],
                 dst_ref=target.at[own],
@@ -456,7 +459,7 @@
             ).start()
             return carry
 
-        lax.fori_loop(1, PEERS, post, 0)
+        lax.fori_loop(0, PEERS - 1, post, 0)
         target[own] = source[slot(own)]
 
     def arrived(target, phase, device):
@@ -475,10 +478,22 @@
     def same(index):
         return index
 
+    def outward(n, middle):
+        return middle + ((n + 1) >> 1) * (1 - 2 * (n & 1))
+
+    def far_first(k):
+        return outward(k, 16)
+
+    def far_plane(k):
+        return (outward(k & 3, 2) & 3) * 8 + (outward(k >> 2, 4) & 7)
+
+    def low_first(k):
+        return PEERS + k + (k >= at_a).astype(jnp.int32) - at_a
+
     loads[0].wait()
     put(send_a, to_z(mesh[...], picks[1536:]))
     pl.semaphore_wait(barrier, 2 * (PEERS - 1) + 2)
-    exchange(send_a, recv_a, 0, peer_a, at_a, same)
+    exchange(send_a, recv_a, 0, peer_a, at_a, same, far_first)
 
     def halo(source, target, n, device):
         return pltpu.make_async_remote_copy(
@@ -521,7 +536,30 @@
 
     lax.fori_loop(0, TILES, home_table, 0, unroll=2)
 
-    pl.delay(2400)
+    def prepare(step, carry):
+        for n in range(2):
+            tile = step * 2 + n
+            is_z = at_z(tile)
+            z_table[tile, :128, 128:] = one_of(is_z, narrow(SLOPE + 8, tile))
+            z_table[tile, 128:, 128:] = one_of(is_z, narrow(Z_LOW + 4, tile))
+            t_x, d_x = rows_of(THETA, tile), rows_of(SLOPE, tile)
+            t_y, d_y = rows_of(THETA + 4, tile), rows_of(SLOPE + 4, tile)
+            is_x, is_y = at(0, side_at, tile), at(1, side_at, tile)
+            xy_table[tile, 0:16] = one_of(is_x, t_x)
+            xy_table[tile, 16:32] = one_of(is_x, d_x)
+            xy_table[tile, 32:48] = one_of(is_y, t_y)
+            xy_table[tile, 48:64] = one_of(is_y, d_y)
+            is_x, is_y = at(0, corner_x, tile), at(1, corner_y, tile)
+            cw_x, cs_x = one_of(is_x, t_x), one_of(is_x, d_x)
+            cw_y, cs_y = one_of(is_y, t_y), one_of(is_y, d_y)
+            xy_table[tile, 64:80] = cs_x * cw_y
+            xy_table[tile, 80:96] = cw_x * cs_y
+            xy_table[tile, 96:112] = cw_x * cw_y
+        return carry
+
+    lax.fori_loop(0, TILES // 2, prepare, 0)
+
+    pl.delay(1000)
     pl.when(y_at == 7)(side[0].start)
     pl.when(y_at == 0)(side[1].start)
 
@@ -539,7 +577,7 @@
     peer_one_b = peer_b(1)[1]
     sent_0 = arrived(recv_a, 0, peer_one_a)
     put(send_b, to_lines_x(taken(recv_a), forward_x[...], part_xc, part_xs, picks[:1024]))
-    exchange(send_b, recv_b, 1, peer_b, at_b, same)
+    exchange(send_b, recv_b, 1, peer_b, at_b, same, far_plane)
     hand_on(1)
     pl.when(y_at != 0)(lambda: hand_on(0))
     pl.when(y_at != 7)(lambda: hand_on(2))
@@ -557,14 +595,14 @@
             picks[1024:1536],
         ),
     )
-    exchange(send_c, recv_c, 2, peer_b, at_b, lambda index: index & 7)
+    exchange(send_c, recv_c, 2, peer_b, at_b, lambda index: index & 7, far_plane)
 
     pl.when(y_at == 0)(lambda: hand_on(0))
     pl.when(y_at == 7)(lambda: hand_on(2))
 
     sent_2 = arrived(recv_c, 2, peer_one_b)
     put(send_d, from_lines_x(taken(recv_c), inverse[:128], part_xc, part_xs, picks[:1024]))
-    exchange(send_d, recv_d, 3, peer_a, at_a, same)
+    exchange(send_d, recv_d, 3, peer_a, at_a, same, low_first)
 
     for copy in ends:
         copy.wait()
@@ -593,28 +631,22 @@
     owners = jnp.where(home_vmem[...] == tile_ids, 1.0, 0.0).astype(bf16)
     for c in range(3):
         high, low = split(pushes[c])
-        short_ref[c] = (dot(owners, high) + dot(owners, low)) * (charge * (32.0 * 2.0 / math.sqrt(256.0)))
+        short_ref[c] = (dot(owners, high) + dot(owners, low)) * charge
 
     sent_3 = arrived(recv_d, 3, peer_one_a)
     pot_high, pot_low = split(from_z(taken(recv_d), picks[1536:]))
-    pot_parts[:128] = pot_high
-    pot_parts[128:] = pot_low
+    pot_parts[:, :128] = pot_high
+    pot_parts[:, 128:] = pot_low
 
     def interpolate(step, carry):
         for n in range(2):
             tile = step * 2 + n
-            is_z = at_z(tile)
-            high = [one_of(is_z, narrow(THETA + 8, tile)), one_of(is_z, narrow(SLOPE + 8, tile))]
-            low = [one_of(is_z, narrow(Z_LOW, tile)), one_of(is_z, narrow(Z_LOW + 4, tile))]
-            full = dot(pot_parts[...], jnp.concatenate(high, axis=1))
-            along = full[:128] + full[128:] + dot(pot_parts[:128], jnp.concatenate(low, axis=1))
+            high, low = z_table[tile, :128], z_table[tile, 128:]
+            along = dot(pot_parts[...], jnp.concatenate([high, high], axis=0))
+            along += dot(pot_parts[:, :128], low)
             value = [along[8 * k : 8 * k + 8, :128] for k in range(16)]
             slope = [along[8 * k : 8 * k + 8, 128:] for k in range(16)]
-            t_x, d_x = rows_of(THETA, tile), rows_of(SLOPE, tile)
-            t_y, d_y = rows_of(THETA + 4, tile), rows_of(SLOPE + 4, tile)
-            is_x, is_y = at(0, side_at, tile), at(1, side_at, tile)
-            w_x, s_x = one_of(is_x, t_x), one_of(is_x, d_x)
-            w_y, s_y = one_of(is_y, t_y), one_of(is_y, d_y)
+            w_x, s_x, w_y, s_y = (xy_table[tile, 16 * k : 16 * k + 16] for k in range(4))
             by_y = [[], [], []]
             for y in range(SIDE):
                 by_y[0].append(across(w_y, y) * value[y])
@@ -625,15 +657,12 @@
                 by_x[0].append(across(s_x, x) * value[x + 3])
                 by_x[1].append(across(w_x, x) * value[x + 3])
                 by_x[2].append(across(w_x, x) * slope[x + 3])
-            is_x, is_y = at(0, corner_x, tile), at(1, corner_y, tile)
-            cw_x, cs_x = one_of(is_x, t_x), one_of(is_x, d_x)
-            cw_y, cs_y = one_of(is_y, t_y), one_of(is_y, d_y)
             ends_x, ends_y = (s_x, w_x, w_x), (w_y, s_y, w_y)
             for c in range(3):
                 total = ends_x[c][:8] * sum(by_y[c][1:], by_y[c][0])
                 total += ends_y[c][:8] * sum(by_x[c][1:], by_x[c][0])
                 own = slope if c == 2 else value
-                corner = (cs_x * cw_y, cw_x * cs_y, cw_x * cw_y)[c]
+                corner = xy_table[tile, 64 + 16 * c : 80 + 16 * c]
                 total += corner[:8] * own[14] + corner[8:] * own[15]
                 grads[c, pl.ds(tile, 1), :] = jnp.sum(total, axis=0, keepdims=True)
         return carry
@@ -641,10 +670,8 @@
     lax.fori_loop(0, TILES // 2, interpolate, 0)
     for sent in (sent_0, sent_1, sent_2, sent_3):
         sent.wait_send()
-    total_atoms = 4 * 16 * 16 * 4096
-    scale = -0.4 * NG / math.sqrt(NG * total_atoms)
     for c in range(3):
-        long_ref[c] = grads[c] * (charge * scale)
+        long_ref[c] = grads[c] * charge
 
 
 def on_device(atoms, pair_home, pair_other, *tables):
@@ -670,7 +697,9 @@
             pltpu.VMEM((3, PAIRS, TILE), f32),
             pltpu.VMEM((TILES, 16, 4 * TILE), bf16),
             pltpu.VMEM((3, TILES, TILE), f32),
-            pltpu.VMEM((2 * NG, NG), bf16),
+            pltpu.VMEM((NG, 2 * NG), bf16),
+            pltpu.VMEM((TILES, 2 * NG, 2 * TILE), bf16),
+            pltpu.VMEM((TILES, 112, TILE), f32),
             message,
             message,
             message,
@@ -692,6 +721,9 @@
         ),
         name="forces",
     )(blocks, homes, others, homes.reshape(1, PAIRS), *tables)
+    total_atoms = 4 * 16 * 16 * TILES * TILE
+    short = short * (32.0 * 2.0 / math.sqrt(256.0))
+    long = long * (-0.4 * NG / math.sqrt(NG * total_atoms))
     return short.reshape(3, 1, 1, TILES * TILE), long.reshape(3, 1, 1, TILES * TILE)
 
 

time: 61.4 us -> 58.4 us (0.951)
  Pallas kernels: 58.6 us -> 56.2 us
  local copies, waits for them, and re-layouts: 1.9 us -> 0.66 us
  other arithmetic: 0 us -> 0.64 us
    pallas_call x1, Pallas kernels: 58.6 us -> 56.2 us  [on_device(): pl.pallas_call(kernel, out_shape=(force, force), in_specs=[hbm] * (4 + le...]
    unnamed x6 -> x4, local copies, waits for them, and re-layouts: 1.9 us -> 0.66 us
    mul x0 -> x1, other arithmetic: none -> 0.64 us  [on_device(): long = long * (-0.4 * NG / math.sqrt(NG * total_atoms))]
where the time goes in v3:
time: 58.4 us; the launch traced here: 58.2 us
  Pallas kernels  56.2 us (96%)
  local copies, waits for them, and re-layouts  0.66 us (1%)
  between operations  0.65 us (1%)
  other arithmetic  0.64 us (1%)
    pallas_call x1, Pallas kernels, on_device(): pl.pallas_call(kernel, out_shape=(force, force), in_specs=[hbm] * (4 + le...  56.2 us

profile of v3, /device:TPU:1, one launch (start us, length us, event | category | flops | bytes accessed | tf_op | source)
XLA Modules:
  0.0 58.2 jit_solution(6761286391074293085)
XLA Ops:
  0.6 0.0 copy-start
  0.6 0.0 copy-start.1
  0.6 0.6 %copy-done = s32[1,1,64]{2,1,0:T(1,128)S(1)} copy-done((s32[1,1,64]{2,1,0:T(1,128)S(1)}, s32[1,1,64]{2,1,0:T(1,128)}, u32[]{:S(2)}) %copy-start) | copy-done | bytes 280
  1.3 0.0 copy-done.1
  1.3 56.2 %forces.1 = (f32[3,32,128]{2,1,0:T(8,128)S(1)}, f32[3,32,128]{2,1,0:T(8,128)S(1)}) custom-call(f32[4,32,128]{2,1,0:T(8,128)} %bitcast.9, s32[64]{0:T(128)S(1)} %bitcast.6, s32[64]{0:T(128)S(1)} %bitcast.8, s32[1,64]{1,0:T(1,128)S(1)} %bitcast.7, bf16[1792,128]{1,0:T(8,128)(2,1)} %constant.14.clone.picks_hbm, bf16[1024,192]{1,0:T(8,128)(2,1)} %constant.15.clone.fx_hbm, ...), custom_call_target="tpu_custom_call" | custom-call | tf_op jit(solution)/shard_map/forces/pallas_call | solution.py:685
  57.5 0.6 %broadcast_multiply_fusion = (f32[3,32,128]{2,1,0:T(8,128)}, f32[3,32,128]{2,1,0:T(8,128)}) fusion(f32[3,32,128]{2,1,0:T(8,128)S(1)} %get-tuple-element.5, f32[3,32,128]{2,1,0:T(8,128)S(1)} %get-tuple-element.4), kind=kLoop, calls=%fused_computation | loop fusion | flops 24576 | bytes 196608 | tf_op jit(solution)/shard_map/mul | solution.py:726
Async XLA Ops:
  0.6 0.7 %copy-start = (s32[1,1,64]{2,1,0:T(1,128)S(1)}, s32[1,1,64]{2,1,0:T(1,128)}, u32[]{:S(2)}) copy-start(s32[1,1,64]{2,1,0:T(1,128)} %param.9) | copy-start | bytes 772
  0.6 0.7 %copy-start.1 = (s32[1,1,64]{2,1,0:T(1,128)S(1)}, s32[1,1,64]{2,1,0:T(1,128)}, u32[]{:S(2)}) copy-start(s32[1,1,64]{2,1,0:T(1,128)} %param.10) | copy-start | bytes 772

commit v4 on v3

--- a/solution.py
+++ b/solution.py
@@ -47,11 +47,11 @@
 
 def spread_columns(turn_c, turn_s, inner):
     count = turn_c.shape[1]
-    out = np.zeros((inner, 2, NG, count, inner))
+    out = np.zeros((inner, 2, 16, count, inner))
     for i in range(inner):
-        out[i, 0, :, :, i] = turn_c
-        out[i, 1, :, :, i] = turn_s
-    return out.reshape(inner * 2 * NG, count * inner)
+        out[i, 0, :, :, i] = turn_c[:16]
+        out[i, 1, :, :, i] = turn_s[:16]
+    return out.reshape(inner * 32, count * inner)
 
 
 def patch_places():
@@ -161,14 +161,33 @@
     return [t == k for k in range(4)]
 
 
+def unfolded(turned, n):
+    rows = turned[32 * n : 32 * n + 16], turned[32 * n + 16 : 32 * n + 32]
+    return tuple(jnp.concatenate([r] * (NG // 16), axis=0) for r in rows)
+
+
+def folded(x):
+    parts = [x[16 * k : 16 * k + 16] for k in range(NG // 16)]
+    while len(parts) > 1:
+        parts = [a + b for a, b in zip(parts[::2], parts[1::2])]
+    return parts[0]
+
+
+def turned_back(table, lines):
+    high, low = split(jnp.concatenate(lines, axis=0))
+    rows = table.shape[0] // 2
+    full = dot(table, high)
+    return full[:rows] + full[rows:] + dot(table[:rows], low)
+
+
 def to_lines_x(got, forward_x, part_c, part_s, pick_x):
     both = jnp.concatenate([got[:64], got[64:]], axis=1)
     turned = dot(forward_x, stacked(both))
     c2, s2 = jnp.concatenate([part_c] * 2, axis=1), jnp.concatenate([part_s] * 2, axis=1)
     out = None
     for j in range(4):
-        q = c2 * turned[j * 256 : j * 256 + 128] + s2 * turned[j * 256 + 128 : j * 256 + 256]
-        high, low = split(q)
+        turn_c, turn_s = unfolded(turned, j)
+        high, low = split(c2 * turn_c + s2 * turn_s)
         pick = pick_x[j * 256 : (j + 1) * 256]
         term = dot(high, pick) + dot(low, pick)
         out = term if out is None else out + term
@@ -178,40 +197,30 @@
 def through_y(got, factor, forward_y, inverse_y, part_c, part_s, pick_y):
     total = (got[:32] + got[32:64]) + (got[64:96] + got[96:])
     turned = dot(forward_y, stacked(total))
-    lines = jnp.concatenate(
-        [
-            part_c * turned[i * 256 : i * 256 + 128] + part_s * turned[i * 256 + 128 : i * 256 + 256]
-            for i in range(4)
-        ],
-        axis=1,
-    )
-    high, low = split(lines)
+    lines = []
+    for i in range(4):
+        turn_c, turn_s = unfolded(turned, i)
+        lines.append(part_c * turn_c + part_s * turn_s)
+    high, low = split(jnp.concatenate(lines, axis=1))
     freq = (dot(high, pick_y) + dot(low, pick_y)) * factor
     high, low = split(freq)
     wide = dot_nt(high, pick_y) + dot_nt(low, pick_y)
-    out = None
+    lines = []
     for i in range(4):
         piece = wide[:, i * 128 : (i + 1) * 128]
-        high, low = split(jnp.concatenate([part_c * piece, part_s * piece], axis=0))
-        table = inverse_y[:, i * 256 : (i + 1) * 256]
-        full = dot(table, high)
-        term = full[:32] + full[32:] + dot(table[:32], low)
-        out = term if out is None else out + term
-    return out
+        lines += [folded(part_c * piece), folded(part_s * piece)]
+    return turned_back(inverse_y, lines)
 
 
 def from_lines_x(got, inverse_x, part_c, part_s, pick_x):
     high, low = split(got)
     c2, s2 = jnp.concatenate([part_c] * 2, axis=1), jnp.concatenate([part_s] * 2, axis=1)
-    out = None
+    lines = []
     for j in range(4):
         pick = pick_x[j * 256 : (j + 1) * 256]
         wide = dot_nt(high, pick) + dot_nt(low, pick)
-        q_high, q_low = split(jnp.concatenate([c2 * wide, s2 * wide], axis=0))
-        table = inverse_x[:, j * 256 : (j + 1) * 256]
-        full = dot(table, q_high)
-        term = full[:64] + full[64:] + dot(table[:64], q_low)
-        out = term if out is None else out + term
+        lines += [folded(c2 * wide), folded(s2 * wide)]
+    out = turned_back(inverse_x, lines)
     return jnp.concatenate([out[:, :128], out[:, 128:]], axis=0)
 
 
@@ -437,7 +446,7 @@
         mesh[...] += wide[:, :128] + wide[:, 128:] + dot_nt(z_low, p_high)
         return carry
 
-    lax.fori_loop(0, TILES // 4, spread, 0)
+    lax.fori_loop(0, TILES // 4, spread, 0, unroll=2)
 
     def put(ref, value):
         for n in range(value.shape[0] // 4):
@@ -635,15 +644,15 @@
 
     sent_3 = arrived(recv_d, 3, peer_one_a)
     pot_high, pot_low = split(from_z(taken(recv_d), picks[1536:]))
-    pot_parts[:, :128] = pot_high
-    pot_parts[:, 128:] = pot_low
+    for n in range(2):
+        pot_parts[:128, 128 * n : 128 * n + 128] = pot_high
+        pot_parts[128:, 128 * n : 128 * n + 128] = pot_low
 
     def interpolate(step, carry):
         for n in range(2):
             tile = step * 2 + n
-            high, low = z_table[tile, :128], z_table[tile, 128:]
-            along = dot(pot_parts[...], jnp.concatenate([high, high], axis=0))
-            along += dot(pot_parts[:, :128], low)
+            wide = dot(pot_parts[...], z_table[tile])
+            along = wide[:128] + wide[128:]
             value = [along[8 * k : 8 * k + 8, :128] for k in range(16)]
             slope = [along[8 * k : 8 * k + 8, 128:] for k in range(16)]
             w_x, s_x, w_y, s_y = (xy_table[tile, 16 * k : 16 * k + 16] for k in range(4))
@@ -667,7 +676,7 @@
                 grads[c, pl.ds(tile, 1), :] = jnp.sum(total, axis=0, keepdims=True)
         return carry
 
-    lax.fori_loop(0, TILES // 2, interpolate, 0)
+    lax.fori_loop(0, TILES // 2, interpolate, 0, unroll=4)
     for sent in (sent_0, sent_1, sent_2, sent_3):
         sent.wait_send()
     for c in range(3):
@@ -697,7 +706,7 @@
             pltpu.VMEM((3, PAIRS, TILE), f32),
             pltpu.VMEM((TILES, 16, 4 * TILE), bf16),
             pltpu.VMEM((3, TILES, TILE), f32),
-            pltpu.VMEM((NG, 2 * NG), bf16),
+            pltpu.VMEM((2 * NG, 2 * NG), bf16),
             pltpu.VMEM((TILES, 2 * NG, 2 * TILE), bf16),
             pltpu.VMEM((TILES, 112, TILE), f32),
             message,
@@ -717,10 +726,15 @@
             pltpu.SemaphoreType.DMA((8,)),
         ],
         compiler_params=pltpu.CompilerParams(
-            collective_id=0, has_side_effects=True, vmem_limit_bytes=56_400_000
+            collective_id=0, has_side_effects=True, vmem_limit_bytes=48 << 20
         ),
         name="forces",
-    )(blocks, homes, others, homes.reshape(1, PAIRS), *tables)
+    )(
+        *(
+            pltpu.with_memory_space_constraint(operand, pltpu.HBM)
+            for operand in (blocks, homes, others, homes.reshape(1, PAIRS), *tables)
+        )
+    )
     total_atoms = 4 * 16 * 16 * TILES * TILE
     short = short * (32.0 * 2.0 / math.sqrt(256.0))
     long = long * (-0.4 * NG / math.sqrt(NG * total_atoms))

time: 58.4 us -> 55.3 us (0.947)
  Pallas kernels: 56.2 us -> 53.9 us
  local copies, waits for them, and re-layouts: 0.66 us -> 0 us
    pallas_call x1, Pallas kernels: 56.2 us -> 53.9 us  [on_device(): pl.pallas_call(kernel, out_shape=(force, force), in_specs=[hbm] * (4 + le...]
    unnamed x4 -> x0, local copies, waits for them, and re-layouts: 0.66 us -> none
where the time goes in v4:
time: 55.3 us; the launch traced here: 55.2 us
  Pallas kernels  53.9 us (97%)
  other arithmetic  0.64 us (1%)
  between operations  0.64 us (1%)
    pallas_call x1, Pallas kernels, on_device(): pl.pallas_call(kernel, out_shape=(force, force), in_specs=[hbm] * (4 + le...  53.9 us

profile of v4, /device:TPU:1, one launch (start us, length us, event | category | flops | bytes accessed | tf_op | source)
XLA Modules:
  0.0 55.2 jit_solution(6113817875089985016)
XLA Ops:
  0.6 53.9 %forces.1 = (f32[3,32,128]{2,1,0:T(8,128)S(1)}, f32[3,32,128]{2,1,0:T(8,128)S(1)}) custom-call(f32[4,32,128]{2,1,0:T(8,128)} %bitcast.6, s32[64]{0:T(128)} %bitcast.9, s32[64]{0:T(128)} %bitcast.11, s32[1,64]{1,0:T(1,128)} %bitcast.10, bf16[1792,128]{1,0:T(8,128)(2,1)} %constant.14.clone.picks_hbm, bf16[128,192]{1,0:T(8,128)(2,1)} %constant.15.clone.fx_hbm, ...), custom_call_target="tpu_custom_call" | custom-call | tf_op jit(solution)/shard_map/forces/pallas_call | solution.py:694
  54.5 0.6 %broadcast_multiply_fusion = (f32[3,32,128]{2,1,0:T(8,128)}, f32[3,32,128]{2,1,0:T(8,128)}) fusion(f32[3,32,128]{2,1,0:T(8,128)S(1)} %get-tuple-element.5, f32[3,32,128]{2,1,0:T(8,128)S(1)} %get-tuple-element.4), kind=kLoop, calls=%fused_computation | loop fusion | flops 24576 | bytes 196608 | tf_op jit(solution)/shard_map/mul | solution.py:740

commit v5 on v4

--- a/solution.py
+++ b/solution.py
@@ -348,13 +348,20 @@
     load_atoms.start()
     barrier = pltpu.get_barrier_semaphore()
 
-    for n in range(1, PEERS):
-        k = 16 + (n >> 1) * (1 if n & 1 else -1)
-        pl.semaphore_signal(barrier, 1, device_id=peer_a(k)[1], device_id_type=MESH)
-    for k in range(1, PEERS):
-        pl.semaphore_signal(barrier, 1, device_id=peer_b(k)[1], device_id_type=MESH)
+    def outward(n, middle):
+        return middle + ((n + 1) >> 1) * (1 - 2 * (n & 1))
+
+    def far_first(k):
+        return outward(k, 16)
+
+    def far_plane(k):
+        return (outward(k & 3, 2) & 3) * 8 + (outward(k >> 2, 4) & 7)
+
     pl.semaphore_signal(barrier, 1, device_id=pen_next, device_id_type=MESH)
     pl.semaphore_signal(barrier, 1, device_id=pen_prev, device_id_type=MESH)
+    for n in range(PEERS - 1):
+        pl.semaphore_signal(barrier, 1, device_id=peer_a(far_first(n))[1], device_id_type=MESH)
+        pl.semaphore_signal(barrier, 1, device_id=peer_b(far_plane(n))[1], device_id_type=MESH)
 
     loads = [
         pltpu.make_async_copy(source, target, table_sems.at[n])
@@ -446,7 +453,7 @@
         mesh[...] += wide[:, :128] + wide[:, 128:] + dot_nt(z_low, p_high)
         return carry
 
-    lax.fori_loop(0, TILES // 4, spread, 0, unroll=2)
+    lax.fori_loop(0, TILES // 4, spread, 0, unroll=4)
 
     def put(ref, value):
         for n in range(value.shape[0] // 4):
@@ -486,15 +493,6 @@
 
     def same(index):
         return index
-
-    def outward(n, middle):
-        return middle + ((n + 1) >> 1) * (1 - 2 * (n & 1))
-
-    def far_first(k):
-        return outward(k, 16)
-
-    def far_plane(k):
-        return (outward(k & 3, 2) & 3) * 8 + (outward(k >> 2, 4) & 7)
 
     def low_first(k):
         return PEERS + k + (k >= at_a).astype(jnp.int32) - at_a

time: 55.3 us -> 54.9 us (level)
  no operation moved by 1% of the time
where the time goes in v5:
time: 54.9 us; the launch traced here: 54.7 us
  Pallas kernels  53.4 us (97%)
  other arithmetic  0.64 us (1%)
  between operations  0.64 us (1%)
    pallas_call x1, Pallas kernels, on_device(): pl.pallas_call(kernel, out_shape=(force, force), in_specs=[hbm] * (4 + le...  53.4 us

profile of v5, /device:TPU:1, one launch (start us, length us, event | category | flops | bytes accessed | tf_op | source)
XLA Modules:
  0.0 54.7 jit_solution(9100125345579069795)
XLA Ops:
  0.6 53.4 %forces.1 = (f32[3,32,128]{2,1,0:T(8,128)S(1)}, f32[3,32,128]{2,1,0:T(8,128)S(1)}) custom-call(f32[4,32,128]{2,1,0:T(8,128)} %bitcast.6, s32[64]{0:T(128)} %bitcast.9, s32[64]{0:T(128)} %bitcast.11, s32[1,64]{1,0:T(1,128)} %bitcast.10, bf16[1792,128]{1,0:T(8,128)(2,1)} %constant.14.clone.picks_hbm, bf16[128,192]{1,0:T(8,128)(2,1)} %constant.15.clone.fx_hbm, ...), custom_call_target="tpu_custom_call" | custom-call | tf_op jit(solution)/shard_map/forces/pallas_call | solution.py:692
  54.1 0.6 %broadcast_multiply_fusion = (f32[3,32,128]{2,1,0:T(8,128)}, f32[3,32,128]{2,1,0:T(8,128)}) fusion(f32[3,32,128]{2,1,0:T(8,128)S(1)} %get-tuple-element.5, f32[3,32,128]{2,1,0:T(8,128)S(1)} %get-tuple-element.4), kind=kLoop, calls=%fused_computation | loop fusion | flops 24576 | bytes 196608 | tf_op jit(solution)/shard_map/mul | solution.py:738
